TPU v7x, 256 devices: a whole 4x4x8 slice. The times are simulated.
256 devices in a mesh: dp: 8 (over z), seq: 32 (over x, y, core).
Axes of the slice: x: 4, y: 4, z: 8, core: 2. Of those that a mesh axis runs over, the one named last changes fastest.
Arguments:
- queries: bfloat16 [8, 8192, 512], P('dp', 'seq'), may hold values from -0.62890625 to 0.62890625
- keys: bfloat16 [8, 8192, 512], P('dp', 'seq'), may hold values from -0.62890625 to 0.62890625
- values: bfloat16 [8, 8192, 512], P('dp', 'seq'), may hold values from -6 to 6
- level_weights: float32 [8, 8, 4, 8192], P('dp', None, None, 'seq'), may hold values from 0.25 to 4
- proj: bfloat16 [512, 2048], P(None, 'seq'), may hold values from -0.25 to 0.25
- out_grad: bfloat16 [8, 8192, 2048], P('dp', 'seq'), may hold values from -0.59765625 to 0.59765625
Outputs:
- attended_out: bfloat16 [8, 8192, 2048], P('dp', 'seq')
- grad_queries: bfloat16 [8, 8192, 512], P('dp', 'seq')
- grad_keys: bfloat16 [8, 8192, 512], P('dp', 'seq')
- grad_values: bfloat16 [8, 8192, 512], P('dp', 'seq')
- grad_levels: float32 [8, 8, 4, 8192], P('dp', None, None, 'seq')
- grad_proj: float32 [512, 2048], P(None, 'seq')
All inputs are finite; a program needn't handle non-finite values.
Results may differ from a plain program's by a relative error of at most 0.0064.
Values may be sent and summed in bfloat16 or wider, within the bound.
A program may use at most 64 MiB of HBM per device.

v0:
```python
import jax
import jax.numpy as jnp
from jax import lax
from jax.sharding import PartitionSpec as P


def partner_2(value, axis, stride):
    mask = 2**stride
    pairs = [(source, source ^ mask) for source in range(lax.axis_size(axis))]
    return lax.ppermute(value, axis, pairs)


def from_everyone(array, axis):
    copies = jnp.broadcast_to(array, (lax.axis_size(axis), *array.shape))
    return lax.all_to_all(copies, axis, split_axis=0, concat_axis=0, tiled=True)


def taken_together(array, axis):
    everything = from_everyone(array, axis)
    return jnp.sum(everything, axis=0)


def level_table(length, stretch, local_bits):
    place = lax.iota(jnp.int32, length)
    blocks = place // stretch
    apart = jnp.bitwise_xor(blocks[:, None], blocks[None, :])
    table = jnp.zeros((length, length), jnp.int32)
    for bit in range(local_bits):
        table = table + (apart >= 1 << bit).astype(jnp.int32)
    causal = place[:, None] >= place[None, :]
    return (table, causal)


def local_weights(lam, table, causal, local_bits):
    weights = jnp.zeros((lam.shape[1], table.shape[0], table.shape[1]), jnp.float32)
    for level in range(local_bits + 1):
        weights = weights + jnp.where(table[None] == level, lam[level][:, :, None], jnp.float32(0))
    return jnp.where(causal[None], weights, jnp.float32(0))


def marked_bit(index, bit):
    return jnp.bitwise_and(jnp.right_shift(index, bit), 1).astype(jnp.float32)


def shards(queries, keys, values, level_weights, proj, out_grad):
    tokens_here = queries.shape[1]
    heads = level_weights.shape[2]
    levels = level_weights.shape[1]
    width = queries.shape[2]
    size = width // heads
    scale = size ** (-0.5)
    span_count = lax.axis_size("seq")
    dev_bits = span_count.bit_length() - 1
    local_bits = levels - 1 - dev_bits
    stretch = tokens_here >> local_bits
    index = lax.axis_index("seq")
    shape = (tokens_here, heads, size)
    query = queries[0].reshape(shape)
    key = keys[0].reshape(shape)
    value = values[0].reshape(shape)
    lam = level_weights[0]
    grad_out = out_grad[0]
    table, causal = level_table(tokens_here, stretch, local_bits)
    scores = jnp.einsum("thd,shd->hts", query, key, preferred_element_type=jnp.float32)
    weights = local_weights(lam, table, causal, local_bits)
    probs = (scale * weights * scores).astype(jnp.bfloat16)
    total = jnp.einsum("hts,shd->thd", probs, value, preferred_element_type=jnp.float32)
    totals = jnp.einsum("shi,shj->hij", key, value, preferred_element_type=jnp.float32)
    running = totals
    states = []
    for bit in range(dev_bits):
        partner = partner_2(running, "seq", bit)
        states.append((marked_bit(index, bit) * partner).astype(jnp.bfloat16))
        running = running + partner
    cross = jnp.zeros_like(total)
    mapped = []
    for bit in range(dev_bits):
        image = jnp.einsum("thi,hij->thj", query, states[bit], preferred_element_type=jnp.float32)
        mapped.append(image)
        cross = cross + lam[local_bits + 1 + bit].T[:, :, None] * image
    attended = (total + scale * cross).astype(jnp.bfloat16).reshape(tokens_here, width)
    full_proj = lax.all_gather(proj, "seq", axis=1, tiled=True)
    out = jnp.dot(attended, full_proj, preferred_element_type=jnp.float32).astype(jnp.bfloat16)
    grad_att = lax.dot_general(
        grad_out, full_proj, (((1,), (1,)), ((), ())), preferred_element_type=jnp.float32
    ).astype(jnp.bfloat16)
    grad_heads = grad_att.reshape(shape)
    dprob = jnp.einsum("thd,shd->hts", grad_heads, value, preferred_element_type=jnp.float32)
    product = jnp.where(causal[None], scale * scores * dprob, jnp.float32(0))
    grads = [
        jnp.sum(jnp.where(table[None] == level, product, jnp.float32(0)), axis=2)
        for level in range(local_bits + 1)
    ]
    dscore = (scale * weights * dprob).astype(jnp.bfloat16)
    grad_q = jnp.einsum("hts,shd->thd", dscore, key, preferred_element_type=jnp.float32)
    grad_k = jnp.einsum("hts,thd->shd", dscore, query, preferred_element_type=jnp.float32)
    grad_v = jnp.einsum("hts,thd->shd", probs, grad_heads, preferred_element_type=jnp.float32)
    updates = []
    for bit in range(dev_bits):
        grads.append(scale * jnp.sum(grad_heads.astype(jnp.float32) * mapped[bit], axis=2).T)
        weighted = (
            scale * lam[local_bits + 1 + bit].T[:, :, None] * grad_heads.astype(jnp.float32)
        ).astype(jnp.bfloat16)
        updates.append(
            jnp.einsum("thi,thj->hij", query, weighted, preferred_element_type=jnp.float32)
        )
        grad_q = grad_q + jnp.einsum(
            "thj,hij->thi", weighted, states[bit], preferred_element_type=jnp.float32
        )
    pending = [marked_bit(index, bit) * updates[bit] for bit in range(dev_bits)]
    carried = jnp.zeros_like(totals)
    for bit in range(dev_bits):
        sending = jnp.stack(pending[bit:])
        arrived = partner_2(sending, "seq", bit)
        carried = carried + (1.0 - marked_bit(index, bit)) * arrived[0]
        for later in range(bit + 1, dev_bits):
            pending[later] = pending[later] + arrived[later - bit]
    returned = carried.astype(jnp.bfloat16)
    grad_k = grad_k + jnp.einsum(
        "shj,hij->shi", value, returned, preferred_element_type=jnp.float32
    )
    grad_v = grad_v + jnp.einsum("shi,hij->shj", key, returned, preferred_element_type=jnp.float32)
    shard = lax.psum_scatter(
        lax.dot_general(
            grad_out, attended, (((0,), (0,)), ((), ())), preferred_element_type=jnp.float32
        ),
        "seq",
        scatter_dimension=0,
        tiled=True,
    )
    shard = taken_together(shard, "dp")
    grad_levels = jnp.stack(grads)[None]
    return (
        out[None],
        grad_q.astype(jnp.bfloat16).reshape(1, tokens_here, width),
        grad_k.astype(jnp.bfloat16).reshape(1, tokens_here, width),
        grad_v.astype(jnp.bfloat16).reshape(1, tokens_here, width),
        grad_levels,
        shard.T,
    )


def solution(mesh):
    return jax.shard_map(
        shards,
        mesh=mesh,
        in_specs=(
            P("dp", "seq", None),
            P("dp", "seq", None),
            P("dp", "seq", None),
            P("dp", None, None, "seq"),
            P(None, "seq"),
            P("dp", "seq", None),
        ),
        out_specs=(
            P("dp", "seq", None),
            P("dp", "seq", None),
            P("dp", "seq", None),
            P("dp", "seq", None),
            P("dp", None, None, "seq"),
            P(None, "seq"),
        ),
        check_vma=False,
    )
```

profile of v0, /device:TPU:8, one launch (start us, length us, event | category | flops | bytes accessed | tf_op | source)
XLA Modules:
  0.0 216.2 jit_solution(3463574984270043745)
XLA Ops:
  9.0 1.1 reshape_squeeze.10
  12.2 2.2 %collective-permute-start.1 = (f32[4,128,128]{2,1,0:T(8,128)S(1)}, f32[4,128,128]{2,1,0:T(8,128)S(1)}, u32[]{:S(2)}, u32[]{:S(2)}) collective-permute-start(f32[4,128,128]{2,1,0:T(8,128)S(1)} %add.139), channel_id=1, source_target_pairs={{0,2},{1,3},{2,0},{3,1},{4,6},{5,7},{6,4},{7,5},{8,10},{9,11},{10,... | collective-permute-start | bytes 786440 | tf_op jit(solution)/shard_map/ppermute | solution.py:10
  14.5 1.3 fusion.49
  15.7 5.7 %collective-permute-done.1 = f32[4,128,128]{2,1,0:T(8,128)S(1)} collective-permute-done((f32[4,128,128]{2,1,0:T(8,128)S(1)}, f32[4,128,128]{2,1,0:T(8,128)S(1)}, u32[]{:S(2)}, u32[]{:S(2)}) %collective-permute-start.1) | collective-permute-done | bytes 262176 | tf_op jit(solution)/shard_map/ppermute | solution.py:10
  21.5 2.0 collective-permute-start.2
  24.4 7.2 %collective-permute-done.2 = f32[4,128,128]{2,1,0:T(8,128)S(1)} collective-permute-done((f32[4,128,128]{2,1,0:T(8,128)S(1)}, f32[4,128,128]{2,1,0:T(8,128)S(1)}, u32[]{:S(2)}, u32[]{:S(2)}) %collective-permute-start.2) | collective-permute-done | bytes 262176 | tf_op jit(solution)/shard_map/ppermute | solution.py:10
  34.6 4.8 %collective-permute-done.3 = f32[4,128,128]{2,1,0:T(8,128)S(1)} collective-permute-done((f32[4,128,128]{2,1,0:T(8,128)S(1)}, f32[4,128,128]{2,1,0:T(8,128)S(1)}, u32[]{:S(2)}, u32[]{:S(2)}) %collective-permute-start.3) | collective-permute-done | bytes 262176 | tf_op jit(solution)/shard_map/ppermute | solution.py:10
  40.2 1.8 collective-permute-start.4
  43.1 20.3 %all-gather.2.cloned.1.call-done = bf16[512,2048]{0,1:T(8,128)(2,1)} async-done(((bf16[512,64]{0,1:T(8,128)(2,1)}), bf16[512,2048]{0,1:T(8,128)(2,1)}) %all-gather.2.cloned.1.call-update) | async-done | bytes 2097168 | tf_op jit(solution)/shard_map/all_gather | solution.py:82
  63.4 3.0 %convolution_convert_fusion.1 = bf16[256,512]{1,0:T(8,128)(2,1)} fusion(bf16[512,2048]{0,1:T(8,128)(2,1)} %all-gather.2.cloned.1.call-done, bf16[1,256,2048]{2,1,0:T(8,128)(2,1)S(1)} %copy-done), kind=kOutput, calls=%fused_computation.36 | convolution fusion | flops 537001984 | bytes 3407872 | tf_op jit(solution)/shard_map/dot_general | solution.py:84
  67.6 1.7 fusion.25
  70.9 2.7 %convolution_bitcast_fusion = f32[2048,512]{0,1:T(8,128)} fusion(bf16[256,512]{0,1:T(8,128)(2,1)S(1)} %bitcast.293, bf16[1,256,2048]{2,1,0:T(8,128)(2,1)S(1)} %copy-done), kind=kOutput, calls=%fused_computation | convolution fusion | flops 536870912 | bytes 5505024 | tf_op jit(solution)/shard_map/dot_general | solution.py:124
  73.6 5.3 %copy.151 = f32[2048,512]{1,0:T(8,128)} copy(f32[2048,512]{0,1:T(8,128)} %convolution_bitcast_fusion) | data formatting | bytes 8388608
  84.2 2.0 select_reduce_fusion
  91.7 1.5 fusion.86
  93.2 19.8 %collective-permute-done.6 = f32[4,4,128,128]{2,3,1,0:T(8,128)S(1)} collective-permute-done((f32[4,4,128,128]{2,3,1,0:T(8,128)S(1)}, f32[4,4,128,128]{2,3,1,0:T(8,128)S(1)}, u32[]{:S(2)}, u32[]{:S(2)}) %collective-permute-start.6) | collective-permute-done | bytes 1048608 | tf_op jit(solution)/shard_map/ppermute | solution.py:10
  113.3 2.3 %collective-permute-start.7 = (f32[3,4,128,128]{2,3,1,0:T(8,128)S(1)}, f32[3,4,128,128]{2,3,1,0:T(8,128)S(1)}, u32[]{:S(2)}, u32[]{:S(2)}) collective-permute-start(f32[3,4,128,128]{2,3,1,0:T(8,128)S(1)} %pad_maximum_fusion.1), channel_id=1, source_target_pairs={{0,4},{1,5},{2,6},{3,7},{4,0},{5,1},{6,2},{7,3},{8,12},{9,13},{10,... | collective-permute-start | bytes 2359304 | tf_op jit(solution)/shard_map/ppermute | solution.py:10
  115.6 1.4 convolution_bitcast_fusion.1
  117.0 1.5 convolution_bitcast_fusion.4
  118.5 17.9 %collective-permute-done.7 = f32[3,4,128,128]{2,3,1,0:T(8,128)S(1)} collective-permute-done((f32[3,4,128,128]{2,3,1,0:T(8,128)S(1)}, f32[3,4,128,128]{2,3,1,0:T(8,128)S(1)}, u32[]{:S(2)}, u32[]{:S(2)}) %collective-permute-start.7) | collective-permute-done | bytes 786464 | tf_op jit(solution)/shard_map/ppermute | solution.py:10
  137.4 34.0 %reduce-scatter.4.cloned.1.call-done = f32[64,512]{1,0:T(8,128)} async-done(((f32[2048,512]{1,0:T(8,128)}), f32[64,512]{1,0:T(8,128)}) %reduce-scatter.4.cloned.1.call-update) | async-done | bytes 131088 | tf_op jit(solution)/shard_map/reduce_scatter | solution.py:123
  171.4 2.0 broadcast_in_dim.126
  173.4 7.1 %all-to-all-start = ((f32[8,64,512]{2,1,0:T(8,128)}), f32[8,64,512]{2,1,0:T(8,128)}, u32[]{:S(2)}, u32[]{:S(2)}) async-start(f32[8,64,512]{2,1,0:T(8,128)} %broadcast_in_dim.126), calls=%async_computation | async-start | bytes 2097152 | tf_op jit(solution)/shard_map/all_to_all | solution.py:15
  181.2 2.0 fusion.11
  183.2 1.1 fusion.27
  184.3 1.6 collective-permute-start.9
  187.3 3.3 %fusion = bf16[1,256,2048]{2,1,0:T(8,128)(2,1)} fusion(bf16[256,512]{0,1:T(8,128)(2,1)S(1)} %bitcast.294, bf16[512,2048]{0,1:T(8,128)(2,1)} %all-gather.2.cloned.1.call-done), kind=kOutput, calls=%fused_computation.2 | convolution fusion | flops 537395200 | bytes 3407872 | tf_op jit(solution)/shard_map/dot_general | solution.py:83
  190.6 1.7 collective-permute-done.9
  192.4 1.3 fusion.30
  194.8 1.3 fusion.9
  196.9 10.5 %all-to-all-done = f32[8,64,512]{2,1,0:T(8,128)} async-done(((f32[8,64,512]{2,1,0:T(8,128)}), f32[8,64,512]{2,1,0:T(8,128)}, u32[]{:S(2)}, u32[]{:S(2)}) %all-to-all-start) | async-done | bytes 1048608 | tf_op jit(solution)/shard_map/all_to_all | solution.py:15
  207.4 2.0 reduce_sum.89
  (143 shorter events, 28.3 us)
Async XLA Ops:
  7.2 56.2 %copy-start = (bf16[1,256,2048]{2,1,0:T(8,128)(2,1)S(1)}, bf16[1,256,2048]{2,1,0:T(8,128)(2,1)}, u32[]{:S(2)}) copy-start(bf16[1,256,2048]{2,1,0:T(8,128)(2,1)} %param.11) | copy-start | bytes 3145732
  7.2 3.5 %copy-start.31 = (f32[1,8,4,256]{3,2,1,0:T(4,128)S(1)}, f32[1,8,4,256]{3,2,1,0:T(4,128)}, u32[]{:S(2)}) copy-start(f32[1,8,4,256]{3,2,1,0:T(4,128)} %param.9) | copy-start | bytes 98308
  7.2 4.1 %copy-start.30 = (bf16[1,256,512]{2,1,0:T(8,128)(2,1)S(1)}, bf16[1,256,512]{2,1,0:T(8,128)(2,1)}, u32[]{:S(2)}) copy-start(bf16[1,256,512]{2,1,0:T(8,128)(2,1)} %param.6) | copy-start | bytes 786436
  7.2 56.2 %all-gather.2.cloned.1.call-start = ((), (), s32[]{:S(2)}) async-start(), calls=%async_computation.2 | async-start | bytes 2162688 | tf_op jit(solution)/shard_map/all_gather | solution.py:82
  7.9 163.5 %reduce-scatter.4.cloned.1.call-start = ((), (), s32[]{:S(2)}) async-start(), calls=%async_computation.3 | async-start | bytes 4325376 | tf_op jit(solution)/shard_map/reduce_scatter | solution.py:123
  9.0 60.3 %copy-start.7 = (bf16[256,4,128]{2,1,0:T(4,128)(2,1)}, bf16[256,4,128]{2,1,0:T(4,128)(2,1)S(1)}, u32[]{:S(2)}) copy-start(bf16[256,4,128]{2,1,0:T(4,128)(2,1)S(1)} %reshape_squeeze.11) | copy-start | bytes 786436
  10.5 1.7 collective-permute-start
  11.2 58.1 %copy-start.38 = (f32[4,256]{1,0:T(4,128)}, f32[4,256]{1,0:T(4,128)S(1)}, u32[]{:S(2)}) copy-start(f32[4,256]{1,0:T(4,128)S(1)} %get-tuple-element.51) | copy-start | bytes 12292
  12.2 11.9 %copy-start.3 = (f32[4,128,128]{2,1,0:T(8,128)}, f32[4,128,128]{2,1,0:T(8,128)S(1)}, u32[]{:S(2)}) copy-start(f32[4,128,128]{2,1,0:T(8,128)S(1)} %collective-permute-done) | copy-start | bytes 786436
  12.2 9.2 %collective-permute-start.1 = (f32[4,128,128]{2,1,0:T(8,128)S(1)}, f32[4,128,128]{2,1,0:T(8,128)S(1)}, u32[]{:S(2)}, u32[]{:S(2)}) collective-permute-start(f32[4,128,128]{2,1,0:T(8,128)S(1)} %add.139), channel_id=1, source_target_pairs={{0,2},{1,3},{2,0},{3,1},{4,6},{5,7},{6,4},{7,5},{8,10},{9,11},{10,... | collective-permute-start | bytes 786440 | tf_op jit(solution)/shard_map/ppermute | solution.py:10
  21.4 11.0 %copy-start.9 = (f32[4,128,128]{2,1,0:T(8,128)}, f32[4,128,128]{2,1,0:T(8,128)S(1)}, u32[]{:S(2)}) copy-start(f32[4,128,128]{2,1,0:T(8,128)S(1)} %collective-permute-done.1) | copy-start | bytes 786436
  21.5 10.1 %collective-permute-start.2 = (f32[4,128,128]{2,1,0:T(8,128)S(1)}, f32[4,128,128]{2,1,0:T(8,128)S(1)}, u32[]{:S(2)}, u32[]{:S(2)}) collective-permute-start(f32[4,128,128]{2,1,0:T(8,128)S(1)} %add.141), channel_id=1, source_target_pairs={{0,4},{1,5},{2,6},{3,7},{4,0},{5,1},{6,2},{7,3},{8,12},{9,13},{10,... | collective-permute-start | bytes 786440 | tf_op jit(solution)/shard_map/ppermute | solution.py:10
  31.5 3.1 %copy-start.11 = (f32[4,128,128]{2,1,0:T(8,128)}, f32[4,128,128]{2,1,0:T(8,128)S(1)}, u32[]{:S(2)}) copy-start(f32[4,128,128]{2,1,0:T(8,128)S(1)} %collective-permute-done.2) | copy-start | bytes 786436
  31.6 7.8 %collective-permute-start.3 = (f32[4,128,128]{2,1,0:T(8,128)S(1)}, f32[4,128,128]{2,1,0:T(8,128)S(1)}, u32[]{:S(2)}, u32[]{:S(2)}) collective-permute-start(f32[4,128,128]{2,1,0:T(8,128)S(1)} %add.143), channel_id=1, source_target_pairs={{0,8},{1,9},{2,10},{3,11},{4,12},{5,13},{6,14},{7,15},{8,0},{9,1},... | collective-permute-start | bytes 786440 | tf_op jit(solution)/shard_map/ppermute | solution.py:10
  39.4 24.0 %copy-start.13 = (f32[4,128,128]{2,1,0:T(8,128)}, f32[4,128,128]{2,1,0:T(8,128)S(1)}, u32[]{:S(2)}) copy-start(f32[4,128,128]{2,1,0:T(8,128)S(1)} %collective-permute-done.3) | copy-start | bytes 786436
  40.2 27.4 %collective-permute-start.4 = (f32[4,128,128]{2,1,0:T(8,128)}, f32[4,128,128]{2,1,0:T(8,128)S(1)}, u32[]{:S(2)}, u32[]{:S(2)}) collective-permute-start(f32[4,128,128]{2,1,0:T(8,128)} %add.145), channel_id=1, source_target_pairs={{0,16},{1,17},{2,18},{3,19},{4,20},{5,21},{6,22},{7,23},{8,24},{9,... | collective-permute-start | bytes 786440 | tf_op jit(solution)/shard_map/ppermute | solution.py:10
  43.1 24.5 %copy-start.15 = (f32[256,4,128]{0,2,1:T(8,128)S(1)}, f32[256,4,128]{0,2,1:T(8,128)}, u32[]{:S(2)}) copy-start(f32[256,4,128]{0,2,1:T(8,128)} %convolution_bitcast_fusion.13) | copy-start | bytes 1572868
  83.9 3.4 %collective-permute-start.5 = (f32[5,4,128,128]{2,3,1,0:T(8,128)}, f32[5,4,128,128]{2,3,1,0:T(8,128)S(1)}, u32[]{:S(2)}, u32[]{:S(2)}) collective-permute-start(f32[5,4,128,128]{2,3,1,0:T(8,128)} %get-tuple-element.63), channel_id=1, source_target_pairs={{0,1},{1,0},{2,3},{3,2},{4,5},{5,4},{6,7},{7,6},{8,9},{9,8},{10,11... | collective-permute-start | bytes 3932168 | tf_op jit(solution)/shard_map/ppermute | solution.py:10
  84.2 3.1 %copy-start.5 = (f32[4,128,128]{2,1,0:T(8,128)S(1)}, f32[4,128,128]{2,1,0:T(8,128)}, u32[]{:S(2)}) copy-start(f32[4,128,128]{2,1,0:T(8,128)} %get-tuple-element.60) | copy-start | bytes 786436
  84.2 3.1 %copy-start.6 = (f32[4,128,128]{2,1,0:T(8,128)S(1)}, f32[4,128,128]{2,1,0:T(8,128)}, u32[]{:S(2)}) copy-start(f32[4,128,128]{2,1,0:T(8,128)} %get-tuple-element.64) | copy-start | bytes 786436
  84.2 3.1 %copy-start.28 = (f32[4,128,128]{2,1,0:T(8,128)S(1)}, f32[4,128,128]{2,1,0:T(8,128)}, u32[]{:S(2)}) copy-start(f32[4,128,128]{2,1,0:T(8,128)} %get-tuple-element.58) | copy-start | bytes 786436
  87.6 3.1 %copy-start.27 = (f32[4,128,128]{2,1,0:T(8,128)S(1)}, f32[4,128,128]{2,1,0:T(8,128)}, u32[]{:S(2)}) copy-start(f32[4,128,128]{2,1,0:T(8,128)} %copy-done.26) | copy-start | bytes 786436
  87.6 25.4 %collective-permute-start.6 = (f32[4,4,128,128]{2,3,1,0:T(8,128)S(1)}, f32[4,4,128,128]{2,3,1,0:T(8,128)S(1)}, u32[]{:S(2)}, u32[]{:S(2)}) collective-permute-start(f32[4,4,128,128]{2,3,1,0:T(8,128)S(1)} %pad_maximum_fusion), channel_id=1, source_target_pairs={{0,2},{1,3},{2,0},{3,1},{4,6},{5,7},{6,4},{7,5},{8,10},{9,11},{10,... | collective-permute-start | bytes 3145736 | tf_op jit(solution)/shard_map/ppermute | solution.py:10
  113.0 23.3 %copy-start.18 = (f32[4,4,128,128]{2,3,1,0:T(8,128)}, f32[4,4,128,128]{2,3,1,0:T(8,128)S(1)}, u32[]{:S(2)}) copy-start(f32[4,4,128,128]{2,3,1,0:T(8,128)S(1)} %collective-permute-done.6) | copy-start | bytes 3145732
  113.2 23.2 %copy-start.1 = (f32[4,128,128]{1,2,0:T(8,128)}, f32[4,128,128]{1,2,0:T(8,128)S(1)}, u32[]{:S(2)}) copy-start(f32[4,128,128]{1,2,0:T(8,128)S(1)} %get-tuple-element.33) | copy-start | bytes 786436
  113.3 23.1 %collective-permute-start.7 = (f32[3,4,128,128]{2,3,1,0:T(8,128)S(1)}, f32[3,4,128,128]{2,3,1,0:T(8,128)S(1)}, u32[]{:S(2)}, u32[]{:S(2)}) collective-permute-start(f32[3,4,128,128]{2,3,1,0:T(8,128)S(1)} %pad_maximum_fusion.1), channel_id=1, source_target_pairs={{0,4},{1,5},{2,6},{3,7},{4,0},{5,1},{6,2},{7,3},{8,12},{9,13},{10,... | collective-permute-start | bytes 2359304 | tf_op jit(solution)/shard_map/ppermute | solution.py:10
  137.4 45.7 %collective-permute-start.8 = (f32[2,4,128,128]{2,3,1,0:T(8,128)}, f32[2,4,128,128]{2,3,1,0:T(8,128)}, u32[]{:S(2)}, u32[]{:S(2)}) collective-permute-start(f32[2,4,128,128]{2,3,1,0:T(8,128)} %pad_maximum_fusion.2), channel_id=1, source_target_pairs={{0,8},{1,9},{2,10},{3,11},{4,12},{5,13},{6,14},{7,15},{8,0},{9,1},... | collective-permute-start | bytes 1572872 | tf_op jit(solution)/shard_map/ppermute | solution.py:10
  173.4 7.7 %copy-start.4 = (f32[4,128,128]{2,1,0:T(8,128)S(1)}, f32[4,128,128]{2,1,0:T(8,128)}, u32[]{:S(2)}) copy-start(f32[4,128,128]{2,1,0:T(8,128)} %copy-done.3) | copy-start | bytes 786436
  173.4 34.0 %all-to-all-start = ((f32[8,64,512]{2,1,0:T(8,128)}), f32[8,64,512]{2,1,0:T(8,128)}, u32[]{:S(2)}, u32[]{:S(2)}) async-start(f32[8,64,512]{2,1,0:T(8,128)} %broadcast_in_dim.126), calls=%async_computation | async-start | bytes 2097152 | tf_op jit(solution)/shard_map/all_to_all | solution.py:15
  183.2 4.1 %copy-start.20 = (bf16[256,4,128]{0,2,1:T(8,128)(2,1)S(1)}, bf16[256,4,128]{0,2,1:T(8,128)(2,1)}, u32[]{:S(2)}) copy-start(bf16[256,4,128]{0,2,1:T(8,128)(2,1)} %copy-done.19) | copy-start | bytes 786436
  184.3 8.1 %collective-permute-start.9 = (f32[1,4,128,128]{2,3,1,0:T(8,128)S(1)}, f32[1,4,128,128]{2,3,1,0:T(8,128)}, u32[]{:S(2)}, u32[]{:S(2)}) collective-permute-start(f32[1,4,128,128]{2,3,1,0:T(8,128)S(1)} %fusion.27), channel_id=1, source_target_pairs={{0,16},{1,17},{2,18},{3,19},{4,20},{5,21},{6,22},{7,23},{8,24},{9,... | collective-permute-start | bytes 786440 | tf_op jit(solution)/shard_map/ppermute | solution.py:10
  190.6 3.0 %copy-start.29 = (f32[256,4,128]{0,2,1:T(8,128)S(1)}, f32[256,4,128]{0,2,1:T(8,128)}, u32[]{:S(2)}) copy-start(f32[256,4,128]{0,2,1:T(8,128)} %convolution_bitcast_fusion.4) | copy-start | bytes 1572868
  (23 other events, 42.5 us)
Sparse Core Ops, SparseCore 0:
  10.6 52.7 all-gather.1
  79.1 92.2 reduce-scatter.3
where the time goes:
time: 217 us; the launch traced here: 216 us
  waiting for transfers between devices  123 us (57%)
  matrix products  35.5 us (16%)
  starting transfers between devices  19.3 us (9%)
  local copies, waits for them, and re-layouts  14.9 us (7%)
  between operations  14.6 us (7%)
  other arithmetic  9.41 us (4%)
    ppermute x10, waiting for transfers between devices, partner_2(): return lax.ppermute(value, axis, pairs)  57.1 us
    reduce_scatter x1, waiting for transfers between devices, shards(): lax.psum_scatter(lax.dot_general(grad_out, attended, (((0,), (0,)), ((),...  34 us
    all_gather x1, waiting for transfers between devices, shards(): full_proj = lax.all_gather(proj, 'seq', axis=1, tiled=True)  20.3 us
    ppermute x10, starting transfers between devices, partner_2(): return lax.ppermute(value, axis, pairs)  12.1 us
    all_to_all x1, waiting for transfers between devices, from_everyone(): return lax.all_to_all(copies, axis, split_axis=0, concat_axis=0, tiled=True)  10.5 us
    unnamed x91, local copies, waits for them, and re-layouts  8.84 us
    all_to_all x1, starting transfers between devices, from_everyone(): return lax.all_to_all(copies, axis, split_axis=0, concat_axis=0, tiled=True)  7.14 us
    dot_general x5, matrix products, shards(): jnp.einsum('thj,hij->thi', weighted, states[bit], preferred_element_type=...  6.11 us
  transfers between devices with their start and end apart: 13, of which 9 were waited for; matrix products, arithmetic and copies ran while one was open for 21% of the time, Pallas kernels for 0%

commit v1 on v0

v1 whole, which is shorter than its diff:
```python
import functools

import jax
import jax.numpy as jnp
from jax import lax
from jax.experimental import pallas as pl
from jax.experimental.pallas import tpu as pltpu
from jax.sharding import PartitionSpec as P

BF = jnp.bfloat16
F32 = jnp.float32
MESH = pl.DeviceIdType.MESH
COL = 8
PIECES = 16


def place():
    s = lax.axis_index("seq")
    bits = [lax.rem(lax.div(s, 2**b), 2) for b in range(5)]
    return s, bits


def flipped(s, bits, mask):
    peer = s
    for b in range(5):
        if mask >> b & 1:
            peer = peer + 2**b * (1 - 2 * bits[b])
    return peer


def chip_offsets(s, bits):
    c, y0, y1, x0, x1 = bits
    dy0, dy1 = 2 * (1 - 2 * y0), 4 * (1 - 2 * y1)
    dx0, dx1 = 8 * (1 - 2 * x0), 16 * (1 - 2 * x1)
    da0, da1 = dy0 * (1 - c) + dx0 * c, dy1 * (1 - c) + dx1 * c
    db0, db1 = dx0 * (1 - c) + dy0 * c, dx1 * (1 - c) + dy1 * c

    def off(a, b):
        return s + (a & 1) * da0 + (a >> 1) * da1 + (b & 1) * db0 + (b >> 1) * db1

    return off


def rows(index, count):
    return pl.ds(pl.multiple_of(index * count, count), count)


def send(src, dst, ssem, rsem, device):
    return pltpu.make_async_remote_copy(
        src_ref=src, dst_ref=dst, send_sem=ssem, recv_sem=rsem, device_id=device, device_id_type=MESH
    )


def greet(devices):
    barrier = pltpu.get_barrier_semaphore()
    for device in devices:
        pl.semaphore_signal(barrier, inc=1, device_id=device, device_id_type=MESH)
    pl.semaphore_wait(barrier, len(devices))


def bit_of(bits, b, mask):
    return 1 - bits[b] if mask >> b & 1 else bits[b]


def kernel_a(
    k_ref, v_ref, shard_ref, full_ref, states_ref,
    tot, col, pair, quad, csum, xin, s3buf, s4buf,
    ag_s, ag_r, c1_s, c1_r, st_s, st_r, x_s, x_r, sib_s, sib_r,
):
    s, bits = place()
    c, y0, y1, x0, x1 = bits
    r = lax.rem(s, COL)
    off = chip_offsets(s, bits)
    greet(
        [{"seq": flipped(s, bits, m)} for m in range(1, 8)]
        + [{"seq": flipped(s, bits, m << 3)} for m in range(1, 4)]
    )
    sibling = {"seq": flipped(s, bits, 1)}
    open_sends = []

    def block(index):
        return full_ref.at[rows(index, 64)]

    def ag(slot, src, index, device):
        cp = send(src, block(index), ag_s.at[slot], ag_r.at[slot], device)
        cp.start()
        open_sends.append(cp)

    def ag_arrived(slot):
        send(shard_ref, block(s), ag_s.at[slot], ag_r.at[slot], sibling).wait_recv()

    full_ref[rows(s, 64)] = shard_ref[...]
    for a in (1, 3, 2):
        ag(a, shard_ref, s, {"seq": off(a, 0)})
    for b in (1, 3):
        ag(4 + b, shard_ref, s, {"seq": off(0, b)})
    ag(20, shard_ref, s, sibling)

    for h in range(4):
        lanes = pl.ds(128 * h, 128)
        tot[pl.ds(128 * h, 128)] = lax.dot_general(
            k_ref[:, lanes], v_ref[:, lanes], (((0,), (0,)), ((), ())), preferred_element_type=F32
        ).astype(BF)
    first = []
    for m in (4, 5, 2, 3, 6, 7, 1):
        peer = flipped(s, bits, m)
        cp = send(tot.at[rows(lax.rem(peer, COL), 64)], col.at[m], c1_s.at[m], c1_r.at[m], {"seq": peer})
        cp.start()
        first.append(cp)
    sib = send(tot, states_ref.at[0], sib_s, sib_r, sibling)

    @pl.when(c == 0)
    def _():
        sib.start()

    for a in (1, 3, 2):
        ag_arrived(a)
        for b in (1, 3):
            ag(4 + 4 * a + b, block(off(a, 0)), off(a, 0), {"seq": off(0, b)})
        ag(20 + 4 * a, block(off(a, 0)), off(a, 0), sibling)

    for cp in first:
        cp.wait_recv()
    col[0] = tot[rows(r, 64)]
    t = [col[m].astype(F32) for m in range(COL)]
    p = [t[2 * i] + t[2 * i + 1] for i in range(4)]
    q = [p[0] + p[1], p[2] + p[3]]
    csum[...] = q[0] + q[1]
    xsend = []
    for m in range(1, 4):
        cp = send(csum, xin.at[m], x_s.at[m], x_r.at[m], {"seq": flipped(s, bits, m << 3)})
        xsend.append(cp)
    x_out = [x0 == 0, x1 == 0, x1 == 0]
    x_into = [x0 == 1, x1 == 1, x1 == 1]
    for cp, cond in zip(xsend, x_out):

        @pl.when(cond)
        def _(cp=cp):
            cp.start()

    for i in range(4):
        pair[i] = p[i].astype(BF)
    for i in range(2):
        quad[i] = q[i].astype(BF)

    mine = rows(r, 64)

    def spread(j, m, src):
        return send(
            src, states_ref.at[j, mine], st_s.at[j, m], st_r.at[j, m], {"seq": flipped(s, bits, m)}
        )

    order = (1, 4, 5, 2, 3, 6, 7)
    early = []
    for m in order:
        early.append((spread(1, m, pair.at[(m >> 1) ^ 1]), bit_of(bits, 1, m) == 1))
        early.append((spread(2, m, quad.at[(m >> 2) ^ 1]), bit_of(bits, 2, m) == 1))
    for cp, cond in early:

        @pl.when(cond)
        def _(cp=cp):
            cp.start()

    have = [c == 1, y0 == 1, y1 == 1, x0 == 1, x1 == 1]
    for j in range(5):

        @pl.when(jnp.logical_not(have[j]))
        def _(j=j):
            states_ref[j] = jnp.zeros((512, 128), BF)

    @pl.when(have[1])
    def _():
        states_ref[1, mine] = pair[1]

    @pl.when(have[2])
    def _():
        states_ref[2, mine] = quad[1]

    def second(a):
        for b in (1, 3):
            ag_arrived(4 + 4 * a + b)
            if (b == 1) == (a < 2):
                ag(4 + 4 * a + 2, block(off(a, b)), off(a, b), {"seq": off(0, 4 - b)})
            ag(20 + 4 * a + b, block(off(a, b)), off(a, b), sibling)

    second(0)

    late3 = [spread(3, m, s3buf) for m in order]
    late4 = [spread(4, m, s4buf) for m in order]

    @pl.when(have[3])
    def _():
        xsend[0].wait_recv()
        s3buf[...] = xin[1].astype(BF)
        for cp in late3:
            cp.start()
        states_ref[3, mine] = s3buf[...]

    @pl.when(have[4])
    def _():
        xsend[1].wait_recv()
        xsend[2].wait_recv()
        s4buf[...] = (xin[2] + xin[3]).astype(BF)
        for cp in late4:
            cp.start()
        states_ref[4, mine] = s4buf[...]

    for a in (1, 3, 2):
        second(a)
    for a in (0, 1, 3, 2):
        ag_arrived(4 + 4 * a + 2)
        ag(20 + 4 * a + 2, block(off(a, 2)), off(a, 2), sibling)

    @pl.when(have[0])
    def _():
        sib.wait_recv()

    @pl.when(c == 0)
    def _():
        sib.wait_send()

    for cp, cond in early:

        @pl.when(cond)
        def _(cp=cp):
            cp.wait_send()

    for j in range(1, 5):

        @pl.when(have[j])
        def _(j=j):
            for m in order:
                spread(j, m, s4buf).wait_recv()
            if j == 3:
                for cp in late3:
                    cp.wait_send()
            if j == 4:
                for cp in late4:
                    cp.wait_send()

    for cp, cond in zip(xsend, x_out):

        @pl.when(cond)
        def _(cp=cp):
            cp.wait_send()

    for cp in first:
        cp.wait_send()
    for a in range(4):
        for b in range(4):
            ag_arrived(20 + 4 * a + b)
    for cp in open_sends:
        cp.wait_send()


def vmem():
    return pl.BlockSpec(memory_space=pltpu.VMEM)


def gather_states(key, value, shard):
    dma = pltpu.SemaphoreType.DMA
    return pl.pallas_call(
        kernel_a,
        out_shape=(
            jax.ShapeDtypeStruct((2048, 512), BF),
            jax.ShapeDtypeStruct((5, 512, 128), BF),
        ),
        in_specs=[vmem()] * 3,
        out_specs=(vmem(), vmem()),
        scratch_shapes=[
            pltpu.VMEM((512, 128), BF),
            pltpu.VMEM((COL, 64, 128), BF),
            pltpu.VMEM((4, 64, 128), BF),
            pltpu.VMEM((2, 64, 128), BF),
            pltpu.VMEM((64, 128), F32),
            pltpu.VMEM((4, 64, 128), F32),
            pltpu.VMEM((64, 128), BF),
            pltpu.VMEM((64, 128), BF),
            dma((36,)), dma((36,)), dma((COL,)), dma((COL,)),
            dma((5, COL)), dma((5, COL)), dma((4,)), dma((4,)), dma, dma,
        ],
        compiler_params=pltpu.CompilerParams(collective_id=0, has_side_effects=True),
        name="gather_states",
    )(key, value, shard)


def kernel_b(
    u_ref, g_ref, ret_ref, gp_ref,
    ucol, asend, xin, rsend, rcol, usib,
    gsib, hbuf, rel, fin, gbuf, xg, zf, zsend, zin, zall,
    u_s, u_r, ux_s, ux_r, ur_s, ur_r, us_s, us_r,
    gs_s, gs_r, rl_s, rl_r, fn_s, fn_r, gx_s, gx_r, z1_s, z1_r, z2_s, z2_r,
):
    s, bits = place()
    c, y0, y1, x0, x1 = bits
    z = lax.axis_index("dp")
    zbits = [lax.rem(lax.div(z, 2**b), 2) for b in range(3)] + [0, 0]
    r = lax.rem(s, COL)
    off = chip_offsets(s, bits)
    greet(
        [{"seq": flipped(s, bits, m)} for m in range(1, 8)]
        + [{"seq": flipped(s, bits, m << 3)} for m in range(1, 4)]
        + [{"dp": flipped(z, zbits, m)} for m in range(1, 8)]
    )
    sib_index = flipped(s, bits, 1)
    sibling = {"seq": sib_index}
    flip = sib_index - s

    gs = []
    for a in (2, 1, 3, 0):
        for b in range(4):
            slot = 4 * b + a
            cp = send(
                g_ref.at[rows(off(a, b) + flip, 64)], gsib.at[slot], gs_s.at[slot], gs_r.at[slot], sibling
            )
            cp.start()
            gs.append(cp)

    order = (4, 5, 2, 3, 6, 7, 1)
    have = [c == 1, y0 == 1, y1 == 1, x0 == 1, x1 == 1]
    usend = send(u_ref.at[0], usib, us_s, us_r, sibling)

    @pl.when(have[0])
    def _():
        usend.start()

    def slice_to(j, m):
        peer = flipped(s, bits, m)
        return send(
            u_ref.at[j, rows(lax.rem(peer, COL), 64)], ucol.at[j - 1, m], u_s.at[j - 1, m], u_r.at[j - 1, m], {"seq": peer}
        )

    for j in (4, 3, 2, 1):

        @pl.when(have[j])
        def _(j=j):
            for m in order:
                slice_to(j, m).start()

    def gs_arrived(a, b):
        slot = 4 * a + b
        send(g_ref.at[pl.ds(0, 64)], gsib.at[slot], gs_s.at[slot], gs_r.at[slot], sibling).wait_recv()

    def h_make(a, b):
        gs_arrived(a, b)
        hbuf[a, b] = (g_ref[rows(off(a, b), 64)].astype(F32) + gsib[4 * a + b].astype(F32)).astype(BF)

    dev_a = {1: {"seq": off(1, 0)}, 3: {"seq": off(3, 0)}}
    for b in range(4):
        h_make(2, b)
    rl = {
        1: send(hbuf.at[2, pl.ds(0, 2)], rel.at[0], rl_s.at[0], rl_r.at[0], dev_a[1]),
        3: send(hbuf.at[2, pl.ds(2, 2)], rel.at[1], rl_s.at[1], rl_r.at[1], dev_a[3]),
    }
    rl[1].start()
    rl[3].start()

    def final(m, half):
        k = 2 * (m // 2) + half
        return send(
            hbuf.at[m, pl.ds(2 * half, 2)], fin.at[m // 2, pl.ds(2 * half, 2)], fn_s.at[k], fn_r.at[k], dev_a[m]
        )

    h_make(1, 0)
    h_make(1, 1)
    f10 = final(1, 0)
    f10.start()
    h_make(3, 2)
    h_make(3, 3)
    f31 = final(3, 1)
    f31.start()

    for j in range(1, 5):
        for m in range(COL):
            if j == 1:
                cond = bit_of(bits, 1, m) == 1
            elif j == 2:
                cond = bit_of(bits, 2, m) == 1
            else:
                cond = have[j]

            @pl.when(cond)
            def _(j=j, m=m):
                if m:
                    slice_to(j, m).wait_recv()
                else:
                    ucol[j - 1, 0] = u_ref[j, rows(r, 64)]

            @pl.when(jnp.logical_not(cond))
            def _(j=j, m=m):
                ucol[j - 1, m] = jnp.zeros((64, 128), BF)

    def total(j, ms):
        value = ucol[j - 1, ms[0]].astype(F32)
        for m in ms[1:]:
            value = value + ucol[j - 1, m].astype(F32)
        return value

    asend[0] = total(3, list(range(COL)))
    asend[1] = total(4, list(range(COL)))
    ux = [
        send(asend.at[0 if m == 1 else 1], xin.at[m], ux_s.at[m], ux_r.at[m], {"seq": flipped(s, bits, m << 3)})
        for m in range(1, 4)
    ]
    ux_out = [x0 == 1, x1 == 1, x1 == 1]
    for cp, cond in zip(ux, ux_out):

        @pl.when(cond)
        def _(cp=cp):
            cp.start()

    for b in range(2):
        h_make(3, b)
    rl[1].wait_recv()
    for b in range(2):
        hbuf[3, b] = (hbuf[3, b].astype(F32) + rel[0, b].astype(F32)).astype(BF)
    f30 = final(3, 0)
    f30.start()
    for b in range(2):
        h_make(1, 2 + b)
    rl[3].wait_recv()
    for b in range(2):
        hbuf[1, 2 + b] = (hbuf[1, 2 + b].astype(F32) + rel[1, b].astype(F32)).astype(BF)
    f11 = final(1, 1)
    f11.start()

    for cp, cond, m in zip(ux, ux_out, range(1, 4)):

        @pl.when(jnp.logical_not(cond))
        def _(cp=cp):
            cp.wait_recv()

        @pl.when(cond)
        def _(m=m):
            xin[m] = jnp.zeros((64, 128), F32)

    far = xin[1] + xin[2] + xin[3]
    for i in range(4):
        near = total(1, [2 * (i ^ 1), 2 * (i ^ 1) + 1])
        k = 4 * ((i >> 1) ^ 1)
        mid = total(2, [k, k + 1, k + 2, k + 3])
        rsend[i] = (far + near + mid).astype(BF)
    mine = rows(r, 64)
    rc = []
    for m in order:
        cp = send(rsend.at[m >> 1], rcol.at[mine], ur_s.at[m], ur_r.at[m], {"seq": flipped(s, bits, m)})
        cp.start()
        rc.append(cp)
    rcol[mine] = rsend[0]

    for b in range(4):
        h_make(0, b)
    for k, cp in ((0, f10), (1, f11), (2, f30), (3, f31)):
        cp.wait_recv()
    for b in range(4):
        gbuf[b] = (hbuf[0, b].astype(F32) + fin[0, b].astype(F32) + fin[1, b].astype(F32)).astype(BF)
    gx = []
    for b in (2, 1, 3):
        cp = send(gbuf.at[b], xg.at[b], gx_s.at[b], gx_r.at[b], {"seq": off(0, b)})
        cp.start()
        gx.append(cp)

    for cp in rc:
        cp.wait_recv()

    @pl.when(c == 0)
    def _():
        usend.wait_recv()

    @pl.when(have[0])
    def _():
        usib[...] = jnp.zeros((512, 128), BF)

    ret_ref[...] = (rcol[...].astype(F32) + usib[...].astype(F32)).astype(BF)

    for cp in gx:
        cp.wait_recv()
    mean = gbuf[0].astype(F32) + xg[1].astype(F32) + xg[2].astype(F32) + xg[3].astype(F32)
    for i in range(8):
        part = mean[16 * (i // 2) : 16 * (i // 2) + 16, 256 * (i % 2) : 256 * (i % 2) + 256]
        zf[i] = part
        zsend[i] = part.astype(BF)
    z1 = []
    for m in (4, 3, 5, 2, 6, 1, 7):
        peer = flipped(z, zbits, m)
        cp = send(zsend.at[peer], zin.at[m], z1_s.at[m], z1_r.at[m], {"dp": peer})
        cp.start()
        z1.append(cp)
    for cp in z1:
        cp.wait_recv()
    value = zf[z]
    for m in range(1, 8):
        value = value + zin[m].astype(F32)
    zall[z] = value.astype(BF)
    z2 = []
    for m in (4, 3, 5, 2, 6, 1, 7):
        cp = send(zall.at[z], zall.at[z], z2_s.at[m], z2_r.at[m], {"dp": flipped(z, zbits, m)})
        cp.start()
        z2.append(cp)
    for cp in z2:
        cp.wait_recv()
    for i in range(8):
        gp_ref[pl.ds(16 * (i // 2), 16), pl.ds(256 * (i % 2), 256)] = zall[i].astype(F32)

    for cp in gs + [rl[1], rl[3], f10, f11, f30, f31] + rc + gx + z1 + z2:
        cp.wait_send()
    for cp, cond in zip(ux, ux_out):

        @pl.when(cond)
        def _(cp=cp):
            cp.wait_send()

    @pl.when(have[0])
    def _():
        usend.wait_send()

    for j in range(1, 5):

        @pl.when(have[j])
        def _(j=j):
            for m in order:
                slice_to(j, m).wait_send()


def return_states(updates, partial):
    dma = pltpu.SemaphoreType.DMA
    return pl.pallas_call(
        kernel_b,
        out_shape=(
            jax.ShapeDtypeStruct((512, 128), BF),
            jax.ShapeDtypeStruct((64, 512), F32),
        ),
        in_specs=[vmem()] * 2,
        out_specs=(vmem(), vmem()),
        scratch_shapes=[
            pltpu.VMEM((4, COL, 64, 128), BF),
            pltpu.VMEM((2, 64, 128), F32),
            pltpu.VMEM((4, 64, 128), F32),
            pltpu.VMEM((4, 64, 128), BF),
            pltpu.VMEM((512, 128), BF),
            pltpu.VMEM((512, 128), BF),
            pltpu.VMEM((PIECES, 64, 512), BF),
            pltpu.VMEM((4, 4, 64, 512), BF),
            pltpu.VMEM((2, 2, 64, 512), BF),
            pltpu.VMEM((2, 4, 64, 512), BF),
            pltpu.VMEM((4, 64, 512), BF),
            pltpu.VMEM((4, 64, 512), BF),
            pltpu.VMEM((8, 16, 256), F32),
            pltpu.VMEM((8, 16, 256), BF),
            pltpu.VMEM((8, 16, 256), BF),
            pltpu.VMEM((8, 16, 256), BF),
            dma((4, COL)), dma((4, COL)), dma((4,)), dma((4,)), dma((COL,)), dma((COL,)), dma, dma,
            dma((PIECES,)), dma((PIECES,)), dma((2,)), dma((2,)), dma((4,)), dma((4,)),
            dma((4,)), dma((4,)), dma((8,)), dma((8,)), dma((8,)), dma((8,)),
        ],
        compiler_params=pltpu.CompilerParams(collective_id=1, has_side_effects=True),
        name="return_states",
    )(updates, partial)


def level_table(length, stretch, local_bits):
    place = lax.iota(jnp.int32, length)
    blocks = place // stretch
    apart = jnp.bitwise_xor(blocks[:, None], blocks[None, :])
    table = jnp.zeros((length, length), jnp.int32)
    for bit in range(local_bits):
        table = table + (apart >= 1 << bit).astype(jnp.int32)
    causal = place[:, None] >= place[None, :]
    return (table, causal)


def local_weights(lam, table, causal, local_bits):
    weights = jnp.zeros((lam.shape[1], table.shape[0], table.shape[1]), jnp.float32)
    for level in range(local_bits + 1):
        weights = weights + jnp.where(table[None] == level, lam[level][:, :, None], jnp.float32(0))
    return jnp.where(causal[None], weights, jnp.float32(0))


def shards(queries, keys, values, level_weights, proj, out_grad):
    tokens_here, width = queries.shape[1:]
    heads, size, dev_bits, local_bits, stretch = 4, 128, 5, 2, 64
    scale = size ** (-0.5)
    shape = (tokens_here, heads, size)
    query = queries[0].reshape(shape)
    key = keys[0].reshape(shape)
    value = values[0].reshape(shape)
    lam = level_weights[0]
    grad_out = out_grad[0]
    full_t, states = gather_states(keys[0], values[0], proj.T)
    states = states.reshape(dev_bits, heads, size, size)
    table, causal = level_table(tokens_here, stretch, local_bits)
    scores = jnp.einsum("thd,shd->hts", query, key, preferred_element_type=jnp.float32)
    weights = local_weights(lam, table, causal, local_bits)
    probs = (scale * weights * scores).astype(jnp.bfloat16)
    total = jnp.einsum("hts,shd->thd", probs, value, preferred_element_type=jnp.float32)
    cross = jnp.zeros_like(total)
    mapped = []
    for bit in range(dev_bits):
        image = jnp.einsum("thi,hij->thj", query, states[bit], preferred_element_type=jnp.float32)
        mapped.append(image)
        cross = cross + lam[local_bits + 1 + bit].T[:, :, None] * image
    attended = (total + scale * cross).astype(jnp.bfloat16).reshape(tokens_here, width)
    out = lax.dot_general(
        attended, full_t, (((1,), (1,)), ((), ())), preferred_element_type=jnp.float32
    ).astype(jnp.bfloat16)
    grad_att = jnp.dot(grad_out, full_t, preferred_element_type=jnp.float32).astype(jnp.bfloat16)
    grad_heads = grad_att.reshape(shape)
    dprob = jnp.einsum("thd,shd->hts", grad_heads, value, preferred_element_type=jnp.float32)
    product = jnp.where(causal[None], scale * scores * dprob, jnp.float32(0))
    grads = [
        jnp.sum(jnp.where(table[None] == level, product, jnp.float32(0)), axis=2)
        for level in range(local_bits + 1)
    ]
    dscore = (scale * weights * dprob).astype(jnp.bfloat16)
    grad_q = jnp.einsum("hts,shd->thd", dscore, key, preferred_element_type=jnp.float32)
    grad_k = jnp.einsum("hts,thd->shd", dscore, query, preferred_element_type=jnp.float32)
    grad_v = jnp.einsum("hts,thd->shd", probs, grad_heads, preferred_element_type=jnp.float32)
    updates = []
    for bit in range(dev_bits):
        grads.append(scale * jnp.sum(grad_heads.astype(jnp.float32) * mapped[bit], axis=2).T)
        weighted = (
            scale * lam[local_bits + 1 + bit].T[:, :, None] * grad_heads.astype(jnp.float32)
        ).astype(jnp.bfloat16)
        updates.append(
            jnp.einsum("thi,thj->hij", query, weighted, preferred_element_type=jnp.float32).astype(BF)
        )
        grad_q = grad_q + jnp.einsum(
            "thj,hij->thi", weighted, states[bit], preferred_element_type=jnp.float32
        )
    partial = lax.dot_general(
        grad_out, attended, (((0,), (0,)), ((), ())), preferred_element_type=jnp.float32
    ).astype(BF)
    returned, shard = return_states(jnp.stack(updates).reshape(dev_bits, width, size), partial)
    returned = returned.reshape(heads, size, size)
    grad_k = grad_k + jnp.einsum(
        "shj,hij->shi", value, returned, preferred_element_type=jnp.float32
    )
    grad_v = grad_v + jnp.einsum("shi,hij->shj", key, returned, preferred_element_type=jnp.float32)
    grad_levels = jnp.stack(grads)[None]
    return (
        out[None],
        grad_q.astype(jnp.bfloat16).reshape(1, tokens_here, width),
        grad_k.astype(jnp.bfloat16).reshape(1, tokens_here, width),
        grad_v.astype(jnp.bfloat16).reshape(1, tokens_here, width),
        grad_levels,
        shard.T,
    )


def solution(mesh):
    return jax.shard_map(
        shards,
        mesh=mesh,
        in_specs=(
            P("dp", "seq", None),
            P("dp", "seq", None),
            P("dp", "seq", None),
            P("dp", None, None, "seq"),
            P(None, "seq"),
            P("dp", "seq", None),
        ),
        out_specs=(
            P("dp", "seq", None),
            P("dp", "seq", None),
            P("dp", "seq", None),
            P("dp", "seq", None),
            P("dp", None, None, "seq"),
            P(None, "seq"),
        ),
        check_vma=False,
    )
```

time: 217 us -> 95.3 us (0.44)
  waiting for transfers between devices: 123 us -> 0 us
  Pallas kernels: 0 us -> 63.9 us
  starting transfers between devices: 19.3 us -> 0 us
  matrix products: 35.5 us -> 19.9 us
  between operations: 14.6 us -> 1.3 us
  other arithmetic: 9.41 us -> 0.3 us
  local copies, waits for them, and re-layouts: 14.9 us -> 9.65 us
    pallas_call x0 -> x2, Pallas kernels: none -> 63.9 us  [the longest x1 40.3 us: return_states(): pl.pallas_call(kernel_b, out_shape=(jax.ShapeDtypeStruct((512, 128), BF),...]
    ppermute x10 -> x0, waiting for transfers between devices: 57.1 us -> none  [partner_2(): return lax.ppermute(value, axis, pairs)]
    reduce_scatter x1 -> x0, waiting for transfers between devices: 34 us -> none  [shards(): lax.psum_scatter(lax.dot_general(grad_out, attended, (((0,), (0,)), ((),...]
    all_gather x1 -> x0, waiting for transfers between devices: 20.3 us -> none  [shards(): full_proj = lax.all_gather(proj, 'seq', axis=1, tiled=True)]
    ppermute x10 -> x0, starting transfers between devices: 12.1 us -> none  [partner_2(): return lax.ppermute(value, axis, pairs)]
    all_to_all x1 -> x0, waiting for transfers between devices: 10.5 us -> none  [from_everyone(): return lax.all_to_all(copies, axis, split_axis=0, concat_axis=0, tiled=True)]
    all_to_all x1 -> x0, starting transfers between devices: 7.14 us -> none  [from_everyone(): return lax.all_to_all(copies, axis, split_axis=0, concat_axis=0, tiled=True)]
    dot_general x5, matrix products: 6.11 us -> 1.15 us  [shards(): jnp.einsum('thj,hij->thi', weighted, states[bit], preferred_element_type=...]
  transfers between devices with their start and end apart: 13 -> 0, of which waited for: 9 -> 0; matrix products, arithmetic and copies ran while one was open for 21% -> 0% of each run, Pallas kernels for 0% -> 0%
where the time goes in v1:
time: 95.3 us; the launch traced here: 95.1 us
  Pallas kernels  63.9 us (67%)
  matrix products  19.9 us (21%)
  local copies, waits for them, and re-layouts  9.65 us (10%)
  between operations  1.3 us (1%)
    pallas_call x1, Pallas kernels, return_states(): pl.pallas_call(kernel_b, out_shape=(jax.ShapeDtypeStruct((512, 128), BF),...  40.3 us
    pallas_call x1, Pallas kernels, gather_states(): pl.pallas_call(kernel_a, out_shape=(jax.ShapeDtypeStruct((2048, 512), BF)...  23.6 us
    unnamed x85, local copies, waits for them, and re-layouts  5.44 us
    dot_general x5, matrix products, shards(): jnp.einsum('thi,hij->thj', query, states[bit], preferred_element_type=jnp...  2.75 us
    dot_general x1, matrix products, shards(): jnp.einsum('hts,thd->shd', dscore, query, preferred_element_type=jnp.floa...  2.63 us
    dot_general x1, matrix products, shards(): jnp.dot(grad_out, full_t, preferred_element_type=jnp.float32)  2.41 us
    dot_general x1, matrix products, shards(): jnp.einsum('hts,shd->thd', probs, value, preferred_element_type=jnp.float32)  2.2 us
    dot_general x1, matrix products, shards(): lax.dot_general(grad_out, attended, (((0,), (0,)), ((), ())), preferred_e...  2.1 us

profile of v1, /device:TPU:8, one launch (start us, length us, event | category | flops | bytes accessed | tf_op | source)
XLA Modules:
  0.0 95.1 jit_solution(2787279394941560755)
XLA Ops:
  0.6 23.6 %gather_states.1 = (bf16[2048,512]{1,0:T(8,128)(2,1)}, bf16[5,512,128]{2,1,0:T(8,128)(2,1)}) custom-call(bf16[256,512]{1,0:T(8,128)(2,1)} %bitcast.228, bf16[256,512]{1,0:T(8,128)(2,1)} %bitcast.227, bf16[64,512]{1,0:T(8,128)(2,1)} %bitcast.239), custom_call_target="tpu_custom_call" | custom-call | tf_op jit(solution)/shard_map/gather_states/pallas_call | solution.py:262
  24.3 2.4 %convolution_convert_fusion.2 = bf16[512,256]{1,0:T(8,128)(2,1)S(1)} fusion(bf16[2048,512]{1,0:T(8,128)(2,1)} %get-tuple-element.11, bf16[1,256,2048]{2,1,0:T(8,128)(2,1)S(1)} %copy-done), kind=kOutput, calls=%fused_computation.37 | convolution fusion | flops 537001984 | bytes 3407872 | tf_op jit(solution)/shard_map/dot_general | solution.py:606
  26.7 0.7 fusion.47
  27.6 0.3 convolution_bitcast_fusion.10
  28.0 0.3 convolution_bitcast_fusion.11
  28.3 0.3 convolution_bitcast_fusion.12
  28.6 0.3 convolution_bitcast_fusion.13
  28.9 0.8 copy-done.1
  29.7 1.7 %fusion.24 = (f32[256,4]{0,1:T(4,128)S(1)}, f32[256,4]{0,1:T(4,128)S(1)}, f32[256,4]{0,1:T(4,128)S(1)}, f32[256,4]{0,1:T(4,128)S(1)}, f32[256,4]{0,1:T(4,128)}, /*index=5*/f32[256,4,128]{0,2,1:T(8,128)}) fusion(bf16[512,256]{1,0:T(8,128)(2,1)S(1)} %convolution_convert_fusion.2, f32[256,4,128]{0,2,1:T(8,128)S(1)} %convolution_bitcast_fusion.10, ...), kind=kOutput, calls=%fused_computation.64 | convolution fusion | flops 34991104 | bytes 3297280 | tf_op jit(solution)/shard_map/thi,hij->thj/dot_general | solution.py:599
  31.4 0.6 slice_bitcast_fusion.7
  32.0 1.7 %reshape_squeeze.11 = bf16[256,4,128]{2,1,0:T(4,128)(2,1)} reshape(bf16[1,256,512]{2,1,0:T(8,128)(2,1)} %param.8) | data formatting | bytes 524288 | tf_op jit(solution)/shard_map/reshape;squeeze | solution.py:586
  33.7 1.0 %reshape_squeeze.10 = bf16[256,4,128]{2,1,0:T(4,128)(2,1)S(1)} reshape(bf16[1,256,512]{2,1,0:T(8,128)(2,1)} %param.7) | data formatting | bytes 524288 | tf_op jit(solution)/shard_map/reshape;squeeze | solution.py:585
  34.7 0.3 fusion.44
  35.0 0.2 fusion.27
  35.3 2.2 %fusion.9 = bf16[256,4,128]{0,2,1:T(8,128)(2,1)S(1)} fusion(f32[256,4,128]{0,2,1:T(8,128)} %get-tuple-element.52, f32[256,4,128]{0,2,1:T(8,128)S(1)} %convolution_bitcast_fusion.10, f32[256,4,128]{0,2,1:T(8,128)S(1)} %convolution_bitcast_fusion.11, f32[256,4,128]{0,2,1:T(8,128)S(1)} %convolution_bitcast_fusion.12, f32[256,4,128]{0,2,1:T(8,128)} %copy-done.1, ...), kind=kOutput, calls=%fused_computation.36 | convolution fusion | flops 71041024 | bytes 4489216 | tf_op jit(solution)/shard_map/hts,shd->thd/dot_general | solution.py:595
  37.6 1.7 %fusion.1 = bf16[1,256,2048]{2,1,0:T(8,128)(2,1)} fusion(bf16[256,512]{0,1:T(8,128)(2,1)S(1)} %bitcast.214, bf16[2048,512]{1,0:T(8,128)(2,1)S(1)} %copy-done.2), kind=kOutput, calls=%fused_computation.3 | convolution fusion | flops 537395200 | bytes 3407872 | tf_op jit(solution)/shard_map/dot_general | solution.py:603
  40.5 0.7 select_reduce_fusion
  41.3 0.6 convolution_bitcast_fusion
  42.0 0.3 fusion.12
  42.2 0.8 copy.52
  43.1 2.6 %convolution_bitcast_fusion.3 = f32[256,4,128]{0,2,1:T(8,128)} fusion(bf16[256,4,128]{0,2,1:T(8,128)(2,1)S(1)} %bitcast.196, f32[4,256,256]{1,2,0:T(8,128)} %copy-done.36, f32[4,256]{1,0:T(4,128)S(1)} %copy-done.33, f32[4,256]{1,0:T(4,128)S(1)} %copy-done.34, f32[4,256]{1,0:T(4,128)S(1)} %copy-done.32, pred[256,256]{0,1:T(8,128)(4,1)S(1)} %copy-done.28, ...), kind=kOutput, calls=%fused_computation.17 | convolution fusion | flops 69468160 | bytes 2109440 | tf_op jit(solution)/shard_map/hts,thd->shd/dot_general | solution.py:616
  46.3 0.2 convolution_convert_fusion.5
  46.5 0.2 convolution_convert_fusion.4
  47.1 0.8 copy-done.16
  47.9 2.1 %fusion.g_ref = bf16[2048,512]{1,0:T(8,128)(2,1)} fusion(bf16[256,512]{0,1:T(8,128)(2,1)S(1)} %bitcast.215, bf16[1,256,2048]{2,1,0:T(8,128)(2,1)S(1)} %copy-done), kind=kOutput, calls=%fused_computation.1 | convolution fusion | flops 537919488 | bytes 3407872 | tf_op jit(solution)/shard_map/dot_general | solution.py:630
  50.0 40.3 %return_states.1 = (bf16[512,128]{1,0:T(8,128)(2,1)}, f32[64,512]{1,0:T(8,128)}) custom-call(bf16[5,512,128]{2,1,0:T(8,128)(2,1)} %copy-done.16, bf16[2048,512]{1,0:T(8,128)(2,1)} %fusion.g_ref), custom_call_target="tpu_custom_call" | custom-call | tf_op jit(solution)/shard_map/return_states/pallas_call | solution.py:527
  90.3 1.3 %fusion.11 = bf16[256,4,128]{0,2,1:T(8,128)(2,1)S(1)} fusion(f32[256,4,128]{0,2,1:T(8,128)} %convolution_bitcast_fusion.3, bf16[4,128,128]{2,1,0:T(8,128)(2,1)} %bitcast.231, bf16[256,4,128]{2,1,0:T(4,128)(2,1)S(1)} %copy-done.15), kind=kOutput, calls=%fused_computation.39 | convolution fusion | flops 33816576 | bytes 1179648 | tf_op jit(solution)/shard_map/shj,hij->shi/dot_general | solution.py:635
  91.7 0.8 copy.53
  92.5 0.6 fusion.46
  93.2 0.3 fusion.10
  93.4 0.8 copy.54
  94.4 0.7 copy.106
  (95 shorter events, 2.4 us)
Async XLA Ops:
  0.6 23.6 %copy-start = (bf16[1,256,2048]{2,1,0:T(8,128)(2,1)S(1)}, bf16[1,256,2048]{2,1,0:T(8,128)(2,1)}, u32[]{:S(2)}) copy-start(bf16[1,256,2048]{2,1,0:T(8,128)(2,1)} %param.11) | copy-start | bytes 3145732
  24.2 2.5 %copy-start.17 = (bf16[5,512,128]{2,1,0:T(8,128)(2,1)S(1)}, bf16[5,512,128]{2,1,0:T(8,128)(2,1)}, u32[]{:S(2)}) copy-start(bf16[5,512,128]{2,1,0:T(8,128)(2,1)} %get-tuple-element.10) | copy-start | bytes 1966084
  24.2 3.2 %copy-start.19 = (bf16[1,256,512]{2,1,0:T(8,128)(2,1)S(1)}, bf16[1,256,512]{2,1,0:T(8,128)(2,1)}, u32[]{:S(2)}) copy-start(bf16[1,256,512]{2,1,0:T(8,128)(2,1)} %param.6) | copy-start | bytes 786436
  27.4 1.5 %copy-start.5 = (bf16[1,512,128]{2,1,0:T(8,128)(2,1)}, bf16[1,512,128]{2,1,0:T(8,128)(2,1)S(1)}, u32[]{:S(2)}) copy-start(bf16[1,512,128]{2,1,0:T(8,128)(2,1)S(1)} %get-tuple-element.32) | copy-start | bytes 393220
  27.4 1.5 %copy-start.7 = (bf16[1,512,128]{2,1,0:T(8,128)(2,1)}, bf16[1,512,128]{2,1,0:T(8,128)(2,1)S(1)}, u32[]{:S(2)}) copy-start(bf16[1,512,128]{2,1,0:T(8,128)(2,1)S(1)} %get-tuple-element.31) | copy-start | bytes 393220
  27.5 2.1 %copy-start.11 = (bf16[1,512,128]{2,1,0:T(8,128)(2,1)S(1)}, bf16[1,512,128]{2,1,0:T(8,128)(2,1)}, u32[]{:S(2)}) copy-start(bf16[1,512,128]{2,1,0:T(8,128)(2,1)} %get-tuple-element.29) | copy-start | bytes 393220
  28.6 2.8 %copy-start.21 = (f32[1,8,4,256]{3,2,1,0:T(4,128)S(1)}, f32[1,8,4,256]{3,2,1,0:T(4,128)}, u32[]{:S(2)}) copy-start(f32[1,8,4,256]{3,2,1,0:T(4,128)} %param.9) | copy-start | bytes 98308
  28.9 0.8 copy-start.1
  35.0 5.5 %copy-start.13 = (f32[4,256,256]{1,2,0:T(8,128)}, f32[4,256,256]{1,2,0:T(8,128)S(1)}, u32[]{:S(2)}) copy-start(f32[4,256,256]{1,2,0:T(8,128)S(1)} %fusion.44) | copy-start | bytes 3145732
  35.3 5.9 %copy-start.23 = (pred[256,256]{0,1:T(8,128)(4,1)}, pred[256,256]{0,1:T(8,128)(4,1)S(1)}, u32[]{:S(2)}) copy-start(pred[256,256]{0,1:T(8,128)(4,1)S(1)} %get-tuple-element.46) | copy-start | bytes 196612
  35.3 5.9 %copy-start.25 = (pred[256,256]{0,1:T(8,128)(4,1)}, pred[256,256]{0,1:T(8,128)(4,1)S(1)}, u32[]{:S(2)}) copy-start(pred[256,256]{0,1:T(8,128)(4,1)S(1)} %get-tuple-element.47) | copy-start | bytes 196612
  35.3 5.9 %copy-start.27 = (pred[256,256]{0,1:T(8,128)(4,1)}, pred[256,256]{0,1:T(8,128)(4,1)S(1)}, u32[]{:S(2)}) copy-start(pred[256,256]{0,1:T(8,128)(4,1)S(1)} %get-tuple-element.48) | copy-start | bytes 196612
  35.3 5.9 %copy-start.29 = (pred[256,256]{0,1:T(8,128)(4,1)}, pred[256,256]{0,1:T(8,128)(4,1)S(1)}, u32[]{:S(2)}) copy-start(pred[256,256]{0,1:T(8,128)(4,1)S(1)} %get-tuple-element.53) | copy-start | bytes 196612
  35.3 2.3 %copy-start.2 = (bf16[2048,512]{1,0:T(8,128)(2,1)S(1)}, bf16[2048,512]{1,0:T(8,128)(2,1)}, u32[]{:S(2)}) copy-start(bf16[2048,512]{1,0:T(8,128)(2,1)} %get-tuple-element.11) | copy-start | bytes 6291460
  37.5 2.1 %copy-start.3 = (bf16[256,4,128]{0,2,1:T(8,128)(2,1)}, bf16[256,4,128]{0,2,1:T(8,128)(2,1)S(1)}, u32[]{:S(2)}) copy-start(bf16[256,4,128]{0,2,1:T(8,128)(2,1)S(1)} %fusion.9) | copy-start | bytes 786436
  37.6 1.8 %copy-start.22 = (f32[1,8,4,256]{3,2,1,0:T(4,128)S(1)}, f32[1,8,4,256]{3,2,1,0:T(4,128)}, u32[]{:S(2)}) copy-start(f32[1,8,4,256]{3,2,1,0:T(4,128)} %param.9) | copy-start | bytes 98308
  37.6 1.8 %copy-start.12 = (bf16[1,512,128]{2,1,0:T(8,128)(2,1)S(1)}, bf16[1,512,128]{2,1,0:T(8,128)(2,1)}, u32[]{:S(2)}) copy-start(bf16[1,512,128]{2,1,0:T(8,128)(2,1)} %get-tuple-element.29) | copy-start | bytes 393220
  37.6 2.0 %copy-start.10 = (bf16[1,512,128]{2,1,0:T(8,128)(2,1)S(1)}, bf16[1,512,128]{2,1,0:T(8,128)(2,1)}, u32[]{:S(2)}) copy-start(bf16[1,512,128]{2,1,0:T(8,128)(2,1)} %copy-done.9) | copy-start | bytes 393220
  37.6 2.2 %copy-start.8 = (bf16[1,512,128]{2,1,0:T(8,128)(2,1)S(1)}, bf16[1,512,128]{2,1,0:T(8,128)(2,1)}, u32[]{:S(2)}) copy-start(bf16[1,512,128]{2,1,0:T(8,128)(2,1)} %copy-done.7) | copy-start | bytes 393220
  39.4 0.9 copy-start.6
  39.4 1.1 %copy-start.15 = (bf16[256,4,128]{2,1,0:T(4,128)(2,1)S(1)}, bf16[256,4,128]{2,1,0:T(4,128)(2,1)}, u32[]{:S(2)}) copy-start(bf16[256,4,128]{2,1,0:T(4,128)(2,1)} %reshape_squeeze.11) | copy-start | bytes 786436
  41.2 1.0 %copy-start.36 = (f32[4,256,256]{1,2,0:T(8,128)}, f32[4,256,256]{1,2,0:T(8,128)S(1)}, u32[]{:S(2)}) copy-start(f32[4,256,256]{1,2,0:T(8,128)S(1)} %get-tuple-element.51) | copy-start | bytes 3145732
  41.9 1.2 %copy-start.24 = (pred[256,256]{0,1:T(8,128)(4,1)S(1)}, pred[256,256]{0,1:T(8,128)(4,1)}, u32[]{:S(2)}) copy-start(pred[256,256]{0,1:T(8,128)(4,1)} %copy-done.23) | copy-start | bytes 196612
  41.9 1.2 %copy-start.26 = (pred[256,256]{0,1:T(8,128)(4,1)S(1)}, pred[256,256]{0,1:T(8,128)(4,1)}, u32[]{:S(2)}) copy-start(pred[256,256]{0,1:T(8,128)(4,1)} %copy-done.25) | copy-start | bytes 196612
  41.9 1.2 %copy-start.28 = (pred[256,256]{0,1:T(8,128)(4,1)S(1)}, pred[256,256]{0,1:T(8,128)(4,1)}, u32[]{:S(2)}) copy-start(pred[256,256]{0,1:T(8,128)(4,1)} %copy-done.27) | copy-start | bytes 196612
  42.0 1.1 %copy-start.30 = (pred[256,256]{0,1:T(8,128)(4,1)S(1)}, pred[256,256]{0,1:T(8,128)(4,1)}, u32[]{:S(2)}) copy-start(pred[256,256]{0,1:T(8,128)(4,1)} %copy-done.29) | copy-start | bytes 196612
  46.0 2.0 %copy-start.4 = (bf16[256,4,128]{0,2,1:T(8,128)(2,1)S(1)}, bf16[256,4,128]{0,2,1:T(8,128)(2,1)}, u32[]{:S(2)}) copy-start(bf16[256,4,128]{0,2,1:T(8,128)(2,1)} %copy-done.3) | copy-start | bytes 786436
  47.1 0.8 copy-start.16
  50.0 42.5 %copy-start.14 = (f32[4,256,256]{1,2,0:T(8,128)S(1)}, f32[4,256,256]{1,2,0:T(8,128)}, u32[]{:S(2)}) copy-start(f32[4,256,256]{1,2,0:T(8,128)} %copy-done.13) | copy-start | bytes 3145732
  91.7 1.5 %copy-start.18 = (bf16[512,128]{1,0:T(8,128)(2,1)S(1)}, bf16[512,128]{1,0:T(8,128)(2,1)}, u32[]{:S(2)}) copy-start(bf16[512,128]{1,0:T(8,128)(2,1)} %get-tuple-element.12) | copy-start | bytes 393220
  92.5 1.8 %copy-start.31 = (f32[256,4]{0,1:T(4,128)S(1)}, f32[256,4]{0,1:T(4,128)}, u32[]{:S(2)}) copy-start(f32[256,4]{0,1:T(4,128)} %get-tuple-element.27) | copy-start | bytes 12292
  92.5 1.9 %copy-start.20 = (f32[64,512]{1,0:T(8,128)S(1)}, f32[64,512]{1,0:T(8,128)}, u32[]{:S(2)}) copy-start(f32[64,512]{1,0:T(8,128)} %get-tuple-element.13) | copy-start | bytes 393220
  (5 other events, 3.6 us)

commit v2 on v0

v2 whole, which is shorter than its diff:
```python
import jax
import jax.numpy as jnp
from jax import lax
from jax.experimental import pallas as pl
from jax.experimental.pallas import tpu as pltpu
from jax.sharding import PartitionSpec as P

BF = jnp.bfloat16
F32 = jnp.float32
MESH = pl.DeviceIdType.MESH
COL = 8
PIECES = 16


def place():
    s = lax.axis_index("seq")
    bits = [lax.rem(lax.div(s, 2**b), 2) for b in range(5)]
    return s, bits


def flipped(s, bits, mask):
    peer = s
    for b in range(5):
        if mask >> b & 1:
            peer = peer + 2**b * (1 - 2 * bits[b])
    return peer


def chip_offsets(s, bits):
    c, y0, y1, x0, x1 = bits
    dy0, dy1 = 2 * (1 - 2 * y0), 4 * (1 - 2 * y1)
    dx0, dx1 = 8 * (1 - 2 * x0), 16 * (1 - 2 * x1)
    da0, da1 = dy0 * (1 - c) + dx0 * c, dy1 * (1 - c) + dx1 * c
    db0, db1 = dx0 * (1 - c) + dy0 * c, dx1 * (1 - c) + dy1 * c

    def off(a, b):
        return s + (a & 1) * da0 + (a >> 1) * da1 + (b & 1) * db0 + (b >> 1) * db1

    return off


def rows(index, count):
    return pl.ds(pl.multiple_of(index * count, count), count)


def send(src, dst, ssem, rsem, device):
    return pltpu.make_async_remote_copy(
        src_ref=src, dst_ref=dst, send_sem=ssem, recv_sem=rsem, device_id=device, device_id_type=MESH
    )


def bit_of(bits, b, mask):
    return 1 - bits[b] if mask >> b & 1 else bits[b]


def dot(x, y, dims):
    return lax.dot_general(x, y, (dims, ((), ())), preferred_element_type=F32)


NN, NT, TN = ((1,), (0,)), ((1,), (1,)), ((0,), (0,))
SCALE = 128**-0.5
ORDER = (4, 5, 2, 3, 6, 7, 1)
TILES = ((0, 0), (1, 1), (1, 0))


def step_kernel(
    q_hbm, k_hbm, v_hbm, lam_ref, proj_ref, og_hbm,
    out_ref, gq_ref, gk_ref, gv_ref, gl_ref, gp_ref,
    q, k, v, og, lamt, glt, shard_buf, full, states, score, prob, att32, att, mapped, ga, wt, gk32, gv32,
    tot, col, pair, quad, csum, xin, s3buf, s4buf,
    ubuf, ucol, asend, uxin, rsend, rcol, usib,
    g32, gbf, gsib, hbuf, rel, fin, gbuf, xg, zf, zsend, zin, zall,
    ld, ag_s, ag_r, c1_s, c1_r, st_s, st_r, x_s, x_r, sib_s, sib_r,
    u_s, u_r, ux_s, ux_r, ur_s, ur_r, us_s, us_r,
    gs_s, gs_r, rl_s, rl_r, fn_s, fn_r, gx_s, gx_r, z1_s, z1_r, z2_s, z2_r,
):
    s, bits = place()
    c, y0, y1, x0, x1 = bits
    z = lax.axis_index("dp")
    zbits = [lax.rem(lax.div(z, 2**b), 2) for b in range(3)] + [0, 0]
    r = lax.rem(s, COL)
    mine = rows(r, 64)
    off = chip_offsets(s, bits)
    have = [c == 1, y0 == 1, y1 == 1, x0 == 1, x1 == 1]
    sib_index = flipped(s, bits, 1)
    sibling = {"seq": sib_index}
    flip = sib_index - s

    loads = [
        pltpu.make_async_copy(src, dst, ld.at[i])
        for i, (src, dst) in enumerate(((k_hbm, k), (v_hbm, v), (q_hbm, q), (og_hbm, og)))
    ]
    for cp in loads:
        cp.start()

    greeted = (
        [{"seq": flipped(s, bits, m)} for m in range(1, 8)]
        + [{"seq": flipped(s, bits, m << 3)} for m in range(1, 4)]
        + [{"dp": flipped(z, zbits, m)} for m in range(1, 8)]
    )
    barrier = pltpu.get_barrier_semaphore()
    for device in greeted:
        pl.semaphore_signal(barrier, inc=1, device_id=device, device_id_type=MESH)

    def lanes(h):
        return pl.ds(128 * h, 128)

    shard_buf[...] = proj_ref[...]
    lamt[...] = lam_ref[...].T
    loads[0].wait()
    loads[1].wait()
    for h in range(4):
        tot[lanes(h)] = dot(k[:, lanes(h)], v[:, lanes(h)], TN).astype(BF)
    pl.semaphore_wait(barrier, len(greeted))

    first = []
    for m in ORDER:
        peer = flipped(s, bits, m)
        cp = send(tot.at[rows(lax.rem(peer, COL), 64)], col.at[m], c1_s.at[m], c1_r.at[m], {"seq": peer})
        cp.start()
        first.append(cp)
    sib = send(tot, states.at[0], sib_s, sib_r, sibling)

    @pl.when(c == 0)
    def _():
        sib.start()

    open_sends = []

    def block(index):
        return full.at[rows(index, 64)]

    def ag(slot, src, index, device):
        cp = send(src, block(index), ag_s.at[slot], ag_r.at[slot], device)
        cp.start()
        open_sends.append(cp)

    def ag_arrived(slot):
        send(shard_buf, block(s), ag_s.at[slot], ag_r.at[slot], sibling).wait_recv()

    full[rows(s, 64)] = shard_buf[...]
    for a in (1, 3, 2):
        ag(a, shard_buf, s, {"seq": off(a, 0)})
    for b in (1, 3):
        ag(4 + b, shard_buf, s, {"seq": off(0, b)})
    ag(20, shard_buf, s, sibling)

    row = lax.broadcasted_iota(jnp.int32, (128, 128), 0)
    column = lax.broadcasted_iota(jnp.int32, (128, 128), 1)
    causal = column <= row
    near = causal & ((row < 64) | (column >= 64))
    far = causal & (row >= 64) & (column < 64)

    def half(i):
        return pl.ds(128 * i, 128)

    def lam(level, h, where):
        return lamt[where, pl.ds(4 * level + h, 1)]

    def weight(h, i, j):
        if i != j:
            return SCALE * lam(2, h, half(i))
        return SCALE * jnp.where(near, lam(0, h, half(i)), jnp.where(far, lam(1, h, half(i)), 0.0))

    def inside(h):
        for n, (i, j) in enumerate(TILES):
            value = dot(q[half(i), lanes(h)], k[half(j), lanes(h)], NT)
            score[h, n] = value
            prob[h, n] = (weight(h, i, j) * value).astype(BF)
        att32[half(0), lanes(h)] = dot(prob[h, 0], v[half(0), lanes(h)], NN)
        att32[half(1), lanes(h)] = dot(prob[h, 1], v[half(1), lanes(h)], NN) + dot(
            prob[h, 2], v[half(0), lanes(h)], NN
        )

    loads[2].wait()
    inside(0)
    inside(1)

    for cp in first:
        cp.wait_recv()
    col[0] = tot[mine]
    t = [col[m].astype(F32) for m in range(COL)]
    p = [t[2 * i] + t[2 * i + 1] for i in range(4)]
    qd = [p[0] + p[1], p[2] + p[3]]
    csum[...] = qd[0] + qd[1]
    xsend = [
        send(csum, xin.at[m], x_s.at[m], x_r.at[m], {"seq": flipped(s, bits, m << 3)}) for m in range(1, 4)
    ]
    x_out = [x0 == 0, x1 == 0, x1 == 0]
    for cp, cond in zip(xsend, x_out):

        @pl.when(cond)
        def _(cp=cp):
            cp.start()

    for i in range(4):
        pair[i] = p[i].astype(BF)
    for i in range(2):
        quad[i] = qd[i].astype(BF)

    def spread(j, m, src):
        return send(src, states.at[j, mine], st_s.at[j, m], st_r.at[j, m], {"seq": flipped(s, bits, m)})

    early = []
    for m in ORDER:
        early.append((spread(1, m, pair.at[(m >> 1) ^ 1]), bit_of(bits, 1, m) == 1))
        early.append((spread(2, m, quad.at[(m >> 2) ^ 1]), bit_of(bits, 2, m) == 1))
    for cp, cond in early:

        @pl.when(cond)
        def _(cp=cp):
            cp.start()

    for j in range(5):

        @pl.when(jnp.logical_not(have[j]))
        def _(j=j):
            states[j] = jnp.zeros((512, 128), BF)

    @pl.when(have[1])
    def _():
        states[1, mine] = pair[1]

    @pl.when(have[2])
    def _():
        states[2, mine] = quad[1]

    inside(2)
    inside(3)

    late3 = [spread(3, m, s3buf) for m in ORDER]
    late4 = [spread(4, m, s4buf) for m in ORDER]

    @pl.when(have[3])
    def _():
        xsend[0].wait_recv()
        s3buf[...] = xin[1].astype(BF)
        for cp in late3:
            cp.start()
        states[3, mine] = s3buf[...]

    @pl.when(have[4])
    def _():
        xsend[1].wait_recv()
        xsend[2].wait_recv()
        s4buf[...] = (xin[2] + xin[3]).astype(BF)
        for cp in late4:
            cp.start()
        states[4, mine] = s4buf[...]

    for a in (1, 3, 2):
        ag_arrived(a)
        for b in (1, 3):
            ag(4 + 4 * a + b, block(off(a, 0)), off(a, 0), {"seq": off(0, b)})
        ag(20 + 4 * a, block(off(a, 0)), off(a, 0), sibling)

    @pl.when(have[0])
    def _():
        sib.wait_recv()

    for j in range(1, 5):

        @pl.when(have[j])
        def _(j=j):
            for m in ORDER:
                spread(j, m, s4buf).wait_recv()

    for h in range(4):
        cross = jnp.zeros((256, 128), F32)
        for j in range(5):
            image = dot(q[:, lanes(h)], states[j, lanes(h)], NN)
            mapped[h, j] = image
            cross = cross + lam(3 + j, h, pl.ds(0, 256)) * image
        att[:, lanes(h)] = (att32[:, lanes(h)] + SCALE * cross).astype(BF)

    loads[3].wait()
    gs = []
    for a in (2, 1, 3, 0):
        for b in range(4):
            chip = lax.div(off(a, b), 2)
            at = rows(chip, 128)
            value = dot(og[:, rows(chip, 128)], att[...], TN)
            g32[at] = value
            gbf[at] = value.astype(BF)
            slot = 4 * b + a
            cp = send(gbf.at[rows(off(a, b) + flip, 64)], gsib.at[slot], gs_s.at[slot], gs_r.at[slot], sibling)
            cp.start()
            gs.append(cp)

    def second(a):
        for b in (1, 3):
            ag_arrived(4 + 4 * a + b)
            if (b == 1) == (a < 2):
                ag(4 + 4 * a + 2, block(off(a, b)), off(a, b), {"seq": off(0, 4 - b)})
            ag(20 + 4 * a + b, block(off(a, b)), off(a, b), sibling)

    for a in (0, 1, 3, 2):
        second(a)

    def h_make(a, b):
        slot = 4 * a + b
        send(gbf.at[pl.ds(0, 64)], gsib.at[slot], gs_s.at[slot], gs_r.at[slot], sibling).wait_recv()
        hbuf[a, b] = (g32[rows(off(a, b), 64)] + gsib[slot].astype(F32)).astype(BF)

    dev_a = {1: {"seq": off(1, 0)}, 3: {"seq": off(3, 0)}}
    for b in range(4):
        h_make(2, b)
    rl = {
        1: send(hbuf.at[2, pl.ds(0, 2)], rel.at[0], rl_s.at[0], rl_r.at[0], dev_a[1]),
        3: send(hbuf.at[2, pl.ds(2, 2)], rel.at[1], rl_s.at[1], rl_r.at[1], dev_a[3]),
    }
    rl[1].start()
    rl[3].start()

    def final(m, part):
        n = 2 * (m // 2) + part
        return send(
            hbuf.at[m, pl.ds(2 * part, 2)], fin.at[m // 2, pl.ds(2 * part, 2)], fn_s.at[n], fn_r.at[n], dev_a[m]
        )

    h_make(1, 0)
    h_make(1, 1)
    f10 = final(1, 0)
    f10.start()
    h_make(3, 2)
    h_make(3, 3)
    f31 = final(3, 1)
    f31.start()

    for a in (0, 1, 3, 2):
        ag_arrived(4 + 4 * a + 2)
        ag(20 + 4 * a + 2, block(off(a, 2)), off(a, 2), sibling)
    for a in range(4):
        for b in range(4):
            ag_arrived(20 + 4 * a + b)
    ga[...] = dot(og[...], full[...], NN).astype(BF)
    for h in range(4):
        g = ga[:, lanes(h)].astype(F32)
        for j in range(5):
            wt[h, j] = (SCALE * lam(3 + j, h, pl.ds(0, 256)) * g).astype(BF)
            ubuf[j, lanes(h)] = dot(q[:, lanes(h)], wt[h, j], TN).astype(BF)

    usend = send(ubuf.at[0], usib, us_s, us_r, sibling)

    @pl.when(have[0])
    def _():
        usend.start()

    def slice_to(j, m):
        peer = flipped(s, bits, m)
        return send(
            ubuf.at[j, rows(lax.rem(peer, COL), 64)],
            ucol.at[j - 1, m],
            u_s.at[j - 1, m],
            u_r.at[j - 1, m],
            {"seq": peer},
        )

    for j in (4, 3, 2, 1):

        @pl.when(have[j])
        def _(j=j):
            for m in ORDER:
                slice_to(j, m).start()

    for b in range(2):
        h_make(3, b)
    rl[1].wait_recv()
    for b in range(2):
        hbuf[3, b] = (hbuf[3, b].astype(F32) + rel[0, b].astype(F32)).astype(BF)
    f30 = final(3, 0)
    f30.start()
    for b in range(2):
        h_make(1, 2 + b)
    rl[3].wait_recv()
    for b in range(2):
        hbuf[1, 2 + b] = (hbuf[1, 2 + b].astype(F32) + rel[1, b].astype(F32)).astype(BF)
    f11 = final(1, 1)
    f11.start()

    place_of = lax.broadcasted_iota(jnp.int32, (128, 128), 1)

    def sums(value):
        return jnp.sum(value, axis=1, keepdims=True)

    def backward(h):
        ds = []
        got = {}
        for n, (i, j) in enumerate(TILES):
            dp = dot(ga[half(i), lanes(h)], v[half(j), lanes(h)], NT)
            ds.append((weight(h, i, j) * dp).astype(BF))
            product = SCALE * score[h, n] * dp
            if i != j:
                got[2, i] = sums(product)
            else:
                got[0, i] = sums(jnp.where(near, product, 0.0))
                got[1, i] = sums(jnp.where(far, product, 0.0))
        for i in range(2):
            g = ga[half(i), lanes(h)].astype(F32)
            acc = glt[half(i)]
            for level in range(8):
                if level > 2:
                    value = SCALE * sums(g * mapped[h, level - 3, half(i)])
                elif (level, i) in got:
                    value = got[level, i]
                else:
                    continue
                acc = jnp.where(place_of == 4 * level + h, value, acc)
            glt[half(i)] = acc
        gq = [dot(ds[0], k[half(0), lanes(h)], NN), dot(ds[1], k[half(1), lanes(h)], NN)]
        gq[1] = gq[1] + dot(ds[2], k[half(0), lanes(h)], NN)
        for i in range(2):
            for j in range(5):
                gq[i] = gq[i] + dot(wt[h, j, half(i)], states[j, lanes(h)], NT)
            gq_ref[half(i), lanes(h)] = gq[i].astype(BF)
        q0, q1 = q[half(0), lanes(h)], q[half(1), lanes(h)]
        g0, g1 = ga[half(0), lanes(h)], ga[half(1), lanes(h)]
        gk32[half(0), lanes(h)] = dot(ds[0], q0, TN) + dot(ds[2], q1, TN)
        gk32[half(1), lanes(h)] = dot(ds[1], q1, TN)
        gv32[half(0), lanes(h)] = dot(prob[h, 0], g0, TN) + dot(prob[h, 2], g1, TN)
        gv32[half(1), lanes(h)] = dot(prob[h, 1], g1, TN)

    glt[...] = jnp.zeros_like(glt)
    backward(0)
    backward(1)

    for j in range(1, 5):
        for m in range(COL):
            cond = bit_of(bits, j, m) == 1 if j < 3 else have[j]

            @pl.when(cond)
            def _(j=j, m=m):
                if m:
                    slice_to(j, m).wait_recv()
                else:
                    ucol[j - 1, 0] = ubuf[j, mine]

            @pl.when(jnp.logical_not(cond))
            def _(j=j, m=m):
                ucol[j - 1, m] = jnp.zeros((64, 128), BF)

    def total(j, ms):
        value = ucol[j - 1, ms[0]].astype(F32)
        for m in ms[1:]:
            value = value + ucol[j - 1, m].astype(F32)
        return value

    asend[0] = total(3, list(range(COL)))
    asend[1] = total(4, list(range(COL)))
    ux = [
        send(asend.at[0 if m == 1 else 1], uxin.at[m], ux_s.at[m], ux_r.at[m], {"seq": flipped(s, bits, m << 3)})
        for m in range(1, 4)
    ]
    ux_out = [x0 == 1, x1 == 1, x1 == 1]
    for cp, cond in zip(ux, ux_out):

        @pl.when(cond)
        def _(cp=cp):
            cp.start()

    for b in range(4):
        h_make(0, b)
    for cp in (f10, f31, f30, f11):
        cp.wait_recv()
    for b in range(4):
        gbuf[b] = (hbuf[0, b].astype(F32) + fin[0, b].astype(F32) + fin[1, b].astype(F32)).astype(BF)
    gx = []
    for b in (2, 1, 3):
        cp = send(gbuf.at[b], xg.at[b], gx_s.at[b], gx_r.at[b], {"seq": off(0, b)})
        cp.start()
        gx.append(cp)

    backward(2)

    for cp, cond, m in zip(ux, ux_out, range(1, 4)):

        @pl.when(jnp.logical_not(cond))
        def _(cp=cp):
            cp.wait_recv()

        @pl.when(cond)
        def _(m=m):
            uxin[m] = jnp.zeros((64, 128), F32)

    beyond = uxin[1] + uxin[2] + uxin[3]
    for i in range(4):
        n = 4 * ((i >> 1) ^ 1)
        rsend[i] = (
            beyond + total(1, [2 * (i ^ 1), 2 * (i ^ 1) + 1]) + total(2, [n, n + 1, n + 2, n + 3])
        ).astype(BF)
    rc = []
    for m in ORDER:
        cp = send(rsend.at[m >> 1], rcol.at[mine], ur_s.at[m], ur_r.at[m], {"seq": flipped(s, bits, m)})
        cp.start()
        rc.append(cp)
    rcol[mine] = rsend[0]

    for cp in gx:
        cp.wait_recv()
    mean = gbuf[0].astype(F32) + xg[1].astype(F32) + xg[2].astype(F32) + xg[3].astype(F32)
    for i in range(8):
        part = mean[16 * (i // 2) : 16 * (i // 2) + 16, 256 * (i % 2) : 256 * (i % 2) + 256]
        zf[i] = part
        zsend[i] = part.astype(BF)
    z1 = []
    for m in ORDER:
        peer = flipped(z, zbits, m)
        cp = send(zsend.at[peer], zin.at[m], z1_s.at[m], z1_r.at[m], {"dp": peer})
        cp.start()
        z1.append(cp)

    backward(3)

    def output(n):
        at = pl.ds(512 * n, 512)
        out_ref[:, at] = dot(att[...], full[at], NT).astype(BF)

    output(0)
    output(1)

    for cp in z1:
        cp.wait_recv()
    value = zf[z]
    for m in range(1, 8):
        value = value + zin[m].astype(F32)
    zall[z] = value.astype(BF)
    z2 = []
    for m in ORDER:
        cp = send(zall.at[z], zall.at[z], z2_s.at[m], z2_r.at[m], {"dp": flipped(z, zbits, m)})
        cp.start()
        z2.append(cp)

    output(2)
    output(3)

    for cp in rc:
        cp.wait_recv()

    @pl.when(c == 0)
    def _():
        usend.wait_recv()

    @pl.when(have[0])
    def _():
        usib[...] = jnp.zeros((512, 128), BF)

    for h in range(4):
        back = (rcol[lanes(h)].astype(F32) + usib[lanes(h)].astype(F32)).astype(BF)
        gk_ref[:, lanes(h)] = (gk32[:, lanes(h)] + dot(v[:, lanes(h)], back, NT)).astype(BF)
        gv_ref[:, lanes(h)] = (gv32[:, lanes(h)] + dot(k[:, lanes(h)], back, NN)).astype(BF)
    gl_ref[...] = glt[...].T[:32]

    for cp in z2:
        cp.wait_recv()
    for i in range(8):
        gp_ref[pl.ds(16 * (i // 2), 16), pl.ds(256 * (i % 2), 256)] = zall[i].astype(F32)

    for cp in first + open_sends + gs + [rl[1], rl[3], f10, f11, f30, f31] + rc + gx + z1 + z2:
        cp.wait_send()
    for cp, cond in early + list(zip(xsend, x_out)) + list(zip(ux, ux_out)):

        @pl.when(cond)
        def _(cp=cp):
            cp.wait_send()

    @pl.when(c == 0)
    def _():
        sib.wait_send()

    @pl.when(have[0])
    def _():
        usend.wait_send()

    for j in range(1, 5):

        @pl.when(have[j])
        def _(j=j):
            for m in ORDER:
                slice_to(j, m).wait_send()
            for cp in {3: late3, 4: late4}.get(j, []):
                cp.wait_send()


def step(query, key, value, lam, proj, grad_out):
    dma = pltpu.SemaphoreType.DMA
    any_space = pl.BlockSpec(memory_space=pl.ANY)
    inner = pl.BlockSpec(memory_space=pltpu.VMEM)
    wide = (256, 512)
    return pl.pallas_call(
        step_kernel,
        out_shape=(
            jax.ShapeDtypeStruct((256, 2048), BF),
            jax.ShapeDtypeStruct(wide, BF),
            jax.ShapeDtypeStruct(wide, BF),
            jax.ShapeDtypeStruct(wide, BF),
            jax.ShapeDtypeStruct((32, 256), F32),
            jax.ShapeDtypeStruct((64, 512), F32),
        ),
        in_specs=[any_space, any_space, any_space, inner, inner, any_space],
        out_specs=(inner,) * 6,
        scratch_shapes=[
            pltpu.VMEM(wide, BF), pltpu.VMEM(wide, BF), pltpu.VMEM(wide, BF),
            pltpu.VMEM((256, 2048), BF),
            pltpu.VMEM((256, 32), F32),
            pltpu.VMEM((256, 128), F32),
            pltpu.VMEM((64, 512), BF),
            pltpu.VMEM((2048, 512), BF),
            pltpu.VMEM((5, 512, 128), BF),
            pltpu.VMEM((4, 3, 128, 128), F32),
            pltpu.VMEM((4, 3, 128, 128), BF),
            pltpu.VMEM(wide, F32),
            pltpu.VMEM(wide, BF),
            pltpu.VMEM((4, 5, 256, 128), F32),
            pltpu.VMEM(wide, BF),
            pltpu.VMEM((4, 5, 256, 128), BF),
            pltpu.VMEM(wide, F32),
            pltpu.VMEM(wide, F32),
            pltpu.VMEM((512, 128), BF),
            pltpu.VMEM((COL, 64, 128), BF),
            pltpu.VMEM((4, 64, 128), BF),
            pltpu.VMEM((2, 64, 128), BF),
            pltpu.VMEM((64, 128), F32),
            pltpu.VMEM((4, 64, 128), F32),
            pltpu.VMEM((64, 128), BF),
            pltpu.VMEM((64, 128), BF),
            pltpu.VMEM((5, 512, 128), BF),
            pltpu.VMEM((4, COL, 64, 128), BF),
            pltpu.VMEM((2, 64, 128), F32),
            pltpu.VMEM((4, 64, 128), F32),
            pltpu.VMEM((4, 64, 128), BF),
            pltpu.VMEM((512, 128), BF),
            pltpu.VMEM((512, 128), BF),
            pltpu.VMEM((2048, 512), F32),
            pltpu.VMEM((2048, 512), BF),
            pltpu.VMEM((PIECES, 64, 512), BF),
            pltpu.VMEM((4, 4, 64, 512), BF),
            pltpu.VMEM((2, 2, 64, 512), BF),
            pltpu.VMEM((2, 4, 64, 512), BF),
            pltpu.VMEM((4, 64, 512), BF),
            pltpu.VMEM((4, 64, 512), BF),
            pltpu.VMEM((8, 16, 256), F32),
            pltpu.VMEM((8, 16, 256), BF),
            pltpu.VMEM((8, 16, 256), BF),
            pltpu.VMEM((8, 16, 256), BF),
            dma((4,)),
            dma((36,)), dma((36,)), dma((COL,)), dma((COL,)),
            dma((5, COL)), dma((5, COL)), dma((4,)), dma((4,)), dma, dma,
            dma((4, COL)), dma((4, COL)), dma((4,)), dma((4,)), dma((COL,)), dma((COL,)), dma, dma,
            dma((PIECES,)), dma((PIECES,)), dma((2,)), dma((2,)), dma((4,)), dma((4,)),
            dma((4,)), dma((4,)), dma((8,)), dma((8,)), dma((8,)), dma((8,)),
        ],
        compiler_params=pltpu.CompilerParams(collective_id=0, has_side_effects=True),
        name="span_step",
    )(query, key, value, lam, proj, grad_out)


def shards(queries, keys, values, level_weights, proj, out_grad):
    out, gq, gk, gv, gl, gp = step(
        queries[0], keys[0], values[0], level_weights[0].reshape(32, 256), proj.T, out_grad[0]
    )
    return out[None], gq[None], gk[None], gv[None], gl.reshape(1, 8, 4, 256), gp.T


def solution(mesh):
    return jax.shard_map(
        shards,
        mesh=mesh,
        in_specs=(
            P("dp", "seq", None),
            P("dp", "seq", None),
            P("dp", "seq", None),
            P("dp", None, None, "seq"),
            P(None, "seq"),
            P("dp", "seq", None),
        ),
        out_specs=(
            P("dp", "seq", None),
            P("dp", "seq", None),
            P("dp", "seq", None),
            P("dp", "seq", None),
            P("dp", None, None, "seq"),
            P(None, "seq"),
        ),
        check_vma=False,
    )
```

time: 217 us -> 70.3 us (0.32)
  waiting for transfers between devices: 123 us -> 0 us
  Pallas kernels: 0 us -> 59.6 us
  matrix products: 35.5 us -> 0 us
  starting transfers between devices: 19.3 us -> 0 us
  between operations: 14.6 us -> 0.65 us
  other arithmetic: 9.41 us -> 0 us
  local copies, waits for them, and re-layouts: 14.9 us -> 8.86 us
    pallas_call x0 -> x1, Pallas kernels: none -> 59.6 us  [step(): pl.pallas_call(step_kernel, out_shape=(jax.ShapeDtypeStruct((256, 2048),...]
    ppermute x10 -> x0, waiting for transfers between devices: 57.1 us -> none  [partner_2(): return lax.ppermute(value, axis, pairs)]
    dot_general x27 -> x0, matrix products: 35.5 us -> none  [the longest x5 6.11 us: shards(): jnp.einsum('thj,hij->thi', weighted, states[bit], preferred_element_type=...]
    reduce_scatter x1 -> x0, waiting for transfers between devices: 34 us -> none  [shards(): lax.psum_scatter(lax.dot_general(grad_out, attended, (((0,), (0,)), ((),...]
    all_gather x1 -> x0, waiting for transfers between devices: 20.3 us -> none  [shards(): full_proj = lax.all_gather(proj, 'seq', axis=1, tiled=True)]
    ppermute x10 -> x0, starting transfers between devices: 12.1 us -> none  [partner_2(): return lax.ppermute(value, axis, pairs)]
    all_to_all x1 -> x0, waiting for transfers between devices: 10.5 us -> none  [from_everyone(): return lax.all_to_all(copies, axis, split_axis=0, concat_axis=0, tiled=True)]
    all_to_all x1 -> x0, starting transfers between devices: 7.14 us -> none  [from_everyone(): return lax.all_to_all(copies, axis, split_axis=0, concat_axis=0, tiled=True)]
  transfers between devices with their start and end apart: 13 -> 0, of which waited for: 9 -> 0; matrix products, arithmetic and copies ran while one was open for 21% -> 0% of each run, Pallas kernels for 0% -> 0%
where the time goes in v2:
time: 70.3 us; the launch traced here: 69.1 us
  Pallas kernels  59.6 us (85%)
  local copies, waits for them, and re-layouts  8.86 us (13%)
    pallas_call x1, Pallas kernels, step(): pl.pallas_call(step_kernel, out_shape=(jax.ShapeDtypeStruct((256, 2048),...  59.6 us
    unnamed x13, local copies, waits for them, and re-layouts  6.09 us

profile of v2, /device:TPU:8, one launch (start us, length us, event | category | flops | bytes accessed | tf_op | source)
XLA Modules:
  0.0 69.1 jit_solution(6741980648127001682)
XLA Ops:
  0.6 1.4 %reshape_squeeze.3.lam_ref = f32[32,256]{1,0:T(8,128)} reshape(f32[1,8,4,256]{3,2,1,0:T(4,128)} %param.9) | data formatting | bytes 65536 | tf_op jit(solution)/shard_map/reshape;squeeze | solution.py:659
  2.0 59.6 %span_step.1 = (bf16[256,2048]{1,0:T(8,128)(2,1)}, bf16[256,512]{1,0:T(8,128)(2,1)}, bf16[256,512]{1,0:T(8,128)(2,1)}, bf16[256,512]{1,0:T(8,128)(2,1)}, f32[32,256]{1,0:T(8,128)}, /*index=5*/f32[64,512]{1,0:T(8,128)}) custom-call(bf16[256,512]{1,0:T(8,128)(2,1)} %bitcast.15, bf16[256,512]{1,0:T(8,128)(2,1)} %bitcast.16, bf16[256,512]{1,0:T(8,128)(2,1)} %bitcast.17, ...), custom_call_target="tpu_custom_call" | custom-call | tf_op jit(solution)/shard_map/span_step/pallas_call | solution.py:589
  61.6 1.4 %reshape.15 = f32[1,8,4,256]{3,2,1,0:T(4,128)} reshape(f32[32,256]{1,0:T(8,128)} %get-tuple-element.16) | data formatting | bytes 65536 | tf_op jit(solution)/shard_map/reshape | solution.py:661
  63.0 0.0 copy-start.2
  63.0 2.3 %copy.17 = bf16[1,256,2048]{2,1,0:T(8,128)(2,1)} copy(bf16[1,256,2048]{2,1,0:T(8,128)(2,1)} %bitcast.10) | data formatting | bytes 2097152
  65.3 0.0 copy-done.2
  65.3 0.0 copy-start.1
  65.3 0.7 %copy.18 = bf16[1,256,512]{2,1,0:T(8,128)(2,1)} copy(bf16[1,256,512]{2,1,0:T(8,128)(2,1)S(1)} %bitcast.14) | data formatting | bytes 524288
  66.0 0.3 copy-done.1
  66.4 0.0 copy-start
  66.4 0.7 %copy.19 = bf16[1,256,512]{2,1,0:T(8,128)(2,1)} copy(bf16[1,256,512]{2,1,0:T(8,128)(2,1)S(1)} %bitcast.13) | data formatting | bytes 524288
  67.1 0.3 copy-done
  67.4 0.0 copy-start.3
  67.4 0.7 %copy.20 = bf16[1,256,512]{2,1,0:T(8,128)(2,1)} copy(bf16[1,256,512]{2,1,0:T(8,128)(2,1)S(1)} %bitcast.12) | data formatting | bytes 524288
  68.1 0.3 copy-done.3
  68.4 0.7 copy.21
Async XLA Ops:
  63.0 2.4 %copy-start.2 = (bf16[256,512]{1,0:T(8,128)(2,1)S(1)}, bf16[256,512]{1,0:T(8,128)(2,1)}, u32[]{:S(2)}) copy-start(bf16[256,512]{1,0:T(8,128)(2,1)} %get-tuple-element.13) | copy-start | bytes 786436
  65.3 1.0 %copy-start.1 = (bf16[256,512]{1,0:T(8,128)(2,1)S(1)}, bf16[256,512]{1,0:T(8,128)(2,1)}, u32[]{:S(2)}) copy-start(bf16[256,512]{1,0:T(8,128)(2,1)} %get-tuple-element.14) | copy-start | bytes 786436
  66.4 1.0 %copy-start = (bf16[256,512]{1,0:T(8,128)(2,1)S(1)}, bf16[256,512]{1,0:T(8,128)(2,1)}, u32[]{:S(2)}) copy-start(bf16[256,512]{1,0:T(8,128)(2,1)} %get-tuple-element.15) | copy-start | bytes 786436
  67.4 1.0 %copy-start.3 = (f32[64,512]{1,0:T(8,128)S(1)}, f32[64,512]{1,0:T(8,128)}, u32[]{:S(2)}) copy-start(f32[64,512]{1,0:T(8,128)} %get-tuple-element.17) | copy-start | bytes 393220

commit v3 on v2

--- a/solution.py
+++ b/solution.py
@@ -66,7 +66,7 @@
 def step_kernel(
     q_hbm, k_hbm, v_hbm, lam_ref, proj_ref, og_hbm,
     out_ref, gq_ref, gk_ref, gv_ref, gl_ref, gp_ref,
-    q, k, v, og, lamt, glt, shard_buf, full, states, score, prob, att32, att, mapped, ga, wt, gk32, gv32,
+    q, k, v, og, ogt, lamt, glt, glrow, shard_buf, full, states, score, prob, att32, att, mapped, ga, wt, gk32, gv32,
     tot, col, pair, quad, csum, xin, s3buf, s4buf,
     ubuf, ucol, asend, uxin, rsend, rcol, usib,
     g32, gbf, gsib, hbuf, rel, fin, gbuf, xg, zf, zsend, zin, zall,
@@ -84,7 +84,6 @@
     have = [c == 1, y0 == 1, y1 == 1, x0 == 1, x1 == 1]
     sib_index = flipped(s, bits, 1)
     sibling = {"seq": sib_index}
-    flip = sib_index - s
 
     loads = [
         pltpu.make_async_copy(src, dst, ld.at[i])
@@ -106,7 +105,9 @@
         return pl.ds(128 * h, 128)
 
     shard_buf[...] = proj_ref[...]
-    lamt[...] = lam_ref[...].T
+    for level in range(8):
+        glrow[pl.ds(4 * level, 4)] = lam_ref[level]
+    lamt[...] = glrow[...].T
     loads[0].wait()
     loads[1].wait()
     for h in range(4):
@@ -138,11 +139,14 @@
     def ag_arrived(slot):
         send(shard_buf, block(s), ag_s.at[slot], ag_r.at[slot], sibling).wait_recv()
 
+    def chip(a, b):
+        return flipped(s, bits, a << 1 | b << 3)
+
     full[rows(s, 64)] = shard_buf[...]
     for a in (1, 3, 2):
-        ag(a, shard_buf, s, {"seq": off(a, 0)})
+        ag(a, shard_buf, s, {"seq": chip(a, 0)})
     for b in (1, 3):
-        ag(4 + b, shard_buf, s, {"seq": off(0, b)})
+        ag(4 + b, shard_buf, s, {"seq": chip(0, b)})
     ag(20, shard_buf, s, sibling)
 
     row = lax.broadcasted_iota(jnp.int32, (128, 128), 0)
@@ -225,8 +229,23 @@
     def _():
         states[2, mine] = quad[1]
 
+    def first_axis(a):
+        ag_arrived(a)
+        for b in (1, 3):
+            ag(4 + 4 * a + b, block(chip(a, 0)), chip(a, 0), {"seq": chip(0, b)})
+        ag(20 + 4 * a, block(chip(a, 0)), chip(a, 0), sibling)
+
+    def second_axis(a):
+        for b in (1, 3):
+            ag_arrived(4 + 4 * a + b)
+            if (b == 1) == (a < 2):
+                ag(4 + 4 * a + 2, block(chip(a, b)), chip(a, b), {"seq": chip(0, 4 - b)})
+            ag(20 + 4 * a + b, block(chip(a, b)), chip(a, b), sibling)
+
+    first_axis(1)
+    first_axis(3)
+
     inside(2)
-    inside(3)
 
     late3 = [spread(3, m, s3buf) for m in ORDER]
     late4 = [spread(4, m, s4buf) for m in ORDER]
@@ -248,11 +267,19 @@
             cp.start()
         states[4, mine] = s4buf[...]
 
-    for a in (1, 3, 2):
-        ag_arrived(a)
-        for b in (1, 3):
-            ag(4 + 4 * a + b, block(off(a, 0)), off(a, 0), {"seq": off(0, b)})
-        ag(20 + 4 * a, block(off(a, 0)), off(a, 0), sibling)
+    first_axis(2)
+    second_axis(0)
+    second_axis(1)
+
+    inside(3)
+    loads[3].wait()
+    for n in range(16):
+        turned = og[:, pl.ds(128 * n, 128)].T
+        ogt[0, n] = turned[:64]
+        ogt[1, n] = turned[64:]
+
+    second_axis(3)
+    second_axis(2)
 
     @pl.when(have[0])
     def _():
@@ -273,34 +300,29 @@
             cross = cross + lam(3 + j, h, pl.ds(0, 256)) * image
         att[:, lanes(h)] = (att32[:, lanes(h)] + SCALE * cross).astype(BF)
 
-    loads[3].wait()
+    other = 1 - c
+    for n in range(4):
+        part = pl.ds(4 * n, 4)
+        gbf[part] = dot(ogt[other, part].reshape(256, 256), att[...], NN).astype(BF).reshape(4, 64, 512)
     gs = []
     for a in (2, 1, 3, 0):
         for b in range(4):
-            chip = lax.div(off(a, b), 2)
-            at = rows(chip, 128)
-            value = dot(og[:, rows(chip, 128)], att[...], TN)
-            g32[at] = value
-            gbf[at] = value.astype(BF)
             slot = 4 * b + a
-            cp = send(gbf.at[rows(off(a, b) + flip, 64)], gsib.at[slot], gs_s.at[slot], gs_r.at[slot], sibling)
+            cp = send(gbf.at[lax.div(off(a, b), 2)], gsib.at[slot], gs_s.at[slot], gs_r.at[slot], sibling)
             cp.start()
             gs.append(cp)
-
-    def second(a):
-        for b in (1, 3):
-            ag_arrived(4 + 4 * a + b)
-            if (b == 1) == (a < 2):
-                ag(4 + 4 * a + 2, block(off(a, b)), off(a, b), {"seq": off(0, 4 - b)})
-            ag(20 + 4 * a + b, block(off(a, b)), off(a, b), sibling)
+    for n in range(4):
+        part = pl.ds(4 * n, 4)
+        g32[part] = dot(ogt[c, part].reshape(256, 256), att[...], NN).reshape(4, 64, 512)
 
     for a in (0, 1, 3, 2):
-        second(a)
+        ag_arrived(4 + 4 * a + 2)
+        ag(20 + 4 * a + 2, block(chip(a, 2)), chip(a, 2), sibling)
 
     def h_make(a, b):
         slot = 4 * a + b
-        send(gbf.at[pl.ds(0, 64)], gsib.at[slot], gs_s.at[slot], gs_r.at[slot], sibling).wait_recv()
-        hbuf[a, b] = (g32[rows(off(a, b), 64)] + gsib[slot].astype(F32)).astype(BF)
+        send(gbf.at[0], gsib.at[slot], gs_s.at[slot], gs_r.at[slot], sibling).wait_recv()
+        hbuf[a, b] = (g32[lax.div(off(a, b), 2)] + gsib[slot].astype(F32)).astype(BF)
 
     dev_a = {1: {"seq": off(1, 0)}, 3: {"seq": off(3, 0)}}
     for b in range(4):
@@ -327,9 +349,6 @@
     f31 = final(3, 1)
     f31.start()
 
-    for a in (0, 1, 3, 2):
-        ag_arrived(4 + 4 * a + 2)
-        ag(20 + 4 * a + 2, block(off(a, 2)), off(a, 2), sibling)
     for a in range(4):
         for b in range(4):
             ag_arrived(20 + 4 * a + b)
@@ -548,7 +567,9 @@
         back = (rcol[lanes(h)].astype(F32) + usib[lanes(h)].astype(F32)).astype(BF)
         gk_ref[:, lanes(h)] = (gk32[:, lanes(h)] + dot(v[:, lanes(h)], back, NT)).astype(BF)
         gv_ref[:, lanes(h)] = (gv32[:, lanes(h)] + dot(k[:, lanes(h)], back, NN)).astype(BF)
-    gl_ref[...] = glt[...].T[:32]
+    glrow[...] = glt[...].T[:32]
+    for level in range(8):
+        gl_ref[level] = glrow[pl.ds(4 * level, 4)]
 
     for cp in z2:
         cp.wait_recv()
@@ -593,7 +614,7 @@
             jax.ShapeDtypeStruct(wide, BF),
             jax.ShapeDtypeStruct(wide, BF),
             jax.ShapeDtypeStruct(wide, BF),
-            jax.ShapeDtypeStruct((32, 256), F32),
+            jax.ShapeDtypeStruct((8, 4, 256), F32),
             jax.ShapeDtypeStruct((64, 512), F32),
         ),
         in_specs=[any_space, any_space, any_space, inner, inner, any_space],
@@ -601,8 +622,10 @@
         scratch_shapes=[
             pltpu.VMEM(wide, BF), pltpu.VMEM(wide, BF), pltpu.VMEM(wide, BF),
             pltpu.VMEM((256, 2048), BF),
+            pltpu.VMEM((2, PIECES, 64, 256), BF),
             pltpu.VMEM((256, 32), F32),
             pltpu.VMEM((256, 128), F32),
+            pltpu.VMEM((32, 256), F32),
             pltpu.VMEM((64, 512), BF),
             pltpu.VMEM((2048, 512), BF),
             pltpu.VMEM((5, 512, 128), BF),
@@ -630,8 +653,8 @@
             pltpu.VMEM((4, 64, 128), BF),
             pltpu.VMEM((512, 128), BF),
             pltpu.VMEM((512, 128), BF),
-            pltpu.VMEM((2048, 512), F32),
-            pltpu.VMEM((2048, 512), BF),
+            pltpu.VMEM((PIECES, 64, 512), F32),
+            pltpu.VMEM((PIECES, 64, 512), BF),
             pltpu.VMEM((PIECES, 64, 512), BF),
             pltpu.VMEM((4, 4, 64, 512), BF),
             pltpu.VMEM((2, 2, 64, 512), BF),
@@ -656,9 +679,9 @@
 
 def shards(queries, keys, values, level_weights, proj, out_grad):
     out, gq, gk, gv, gl, gp = step(
-        queries[0], keys[0], values[0], level_weights[0].reshape(32, 256), proj.T, out_grad[0]
+        queries[0], keys[0], values[0], level_weights[0], proj.T, out_grad[0]
     )
-    return out[None], gq[None], gk[None], gv[None], gl.reshape(1, 8, 4, 256), gp.T
+    return out[None], gq[None], gk[None], gv[None], gl[None], gp.T
 
 
 def solution(mesh):

time: 70.3 us -> 64.5 us (0.917)
  the two profiles are of different devices: /device:TPU:8 before, /device:TPU:16 now
where the time goes in v3:
time: 64.5 us; the launch traced here: 64.2 us
  Pallas kernels  57.1 us (89%)
  local copies, waits for them, and re-layouts  6.47 us (10%)
  between operations  0.66 us (1%)
    pallas_call x1, Pallas kernels, step(): pl.pallas_call(step_kernel, out_shape=(jax.ShapeDtypeStruct((256, 2048),...  57.1 us
    unnamed x16, local copies, waits for them, and re-layouts  6.47 us

profile of v3, /device:TPU:16, one launch (start us, length us, event | category | flops | bytes accessed | tf_op | source)
XLA Modules:
  0.0 64.2 jit_solution(10307688675254555745)
XLA Ops:
  0.6 57.1 %span_step.1 = (bf16[256,2048]{1,0:T(8,128)(2,1)}, bf16[256,512]{1,0:T(8,128)(2,1)}, bf16[256,512]{1,0:T(8,128)(2,1)}, bf16[256,512]{1,0:T(8,128)(2,1)}, f32[8,4,256]{2,1,0:T(4,128)}, /*index=5*/f32[64,512]{1,0:T(8,128)}) custom-call(bf16[256,512]{1,0:T(8,128)(2,1)} %bitcast.17, bf16[256,512]{1,0:T(8,128)(2,1)} %bitcast.18, bf16[256,512]{1,0:T(8,128)(2,1)} %bitcast.19, ...), custom_call_target="tpu_custom_call" | custom-call | tf_op jit(solution)/shard_map/span_step/pallas_call | solution.py:610
  57.7 0.0 copy-start.2
  57.7 2.3 %copy.18 = bf16[1,256,2048]{2,1,0:T(8,128)(2,1)} copy(bf16[1,256,2048]{2,1,0:T(8,128)(2,1)} %bitcast.12) | data formatting | bytes 2097152
  60.1 0.0 copy-done.2
  60.1 0.0 copy-start.1
  60.1 0.7 %copy.19 = bf16[1,256,512]{2,1,0:T(8,128)(2,1)} copy(bf16[1,256,512]{2,1,0:T(8,128)(2,1)S(1)} %bitcast.16) | data formatting | bytes 524288
  60.8 0.3 copy-done.1
  61.1 0.0 copy-start
  61.1 0.7 %copy.20 = bf16[1,256,512]{2,1,0:T(8,128)(2,1)} copy(bf16[1,256,512]{2,1,0:T(8,128)(2,1)S(1)} %bitcast.15) | data formatting | bytes 524288
  61.8 0.3 copy-done
  62.2 0.0 copy-start.4
  62.2 0.0 copy-start.3
  62.2 0.7 %copy.21 = bf16[1,256,512]{2,1,0:T(8,128)(2,1)} copy(bf16[1,256,512]{2,1,0:T(8,128)(2,1)S(1)} %bitcast.14) | data formatting | bytes 524288
  62.9 0.1 copy-done.4
  62.9 0.6 copy.22
  63.5 0.0 copy-done.3
  63.6 0.7 %copy.23 = f32[512,64]{0,1:T(8,128)} copy(f32[512,64]{0,1:T(8,128)S(1)} %bitcast.20) | data formatting | bytes 262144
Async XLA Ops:
  57.7 2.4 %copy-start.2 = (bf16[256,512]{1,0:T(8,128)(2,1)S(1)}, bf16[256,512]{1,0:T(8,128)(2,1)}, u32[]{:S(2)}) copy-start(bf16[256,512]{1,0:T(8,128)(2,1)} %get-tuple-element.13) | copy-start | bytes 786436
  60.1 1.0 %copy-start.1 = (bf16[256,512]{1,0:T(8,128)(2,1)S(1)}, bf16[256,512]{1,0:T(8,128)(2,1)}, u32[]{:S(2)}) copy-start(bf16[256,512]{1,0:T(8,128)(2,1)} %get-tuple-element.14) | copy-start | bytes 786436
  61.1 1.0 %copy-start = (bf16[256,512]{1,0:T(8,128)(2,1)S(1)}, bf16[256,512]{1,0:T(8,128)(2,1)}, u32[]{:S(2)}) copy-start(bf16[256,512]{1,0:T(8,128)(2,1)} %get-tuple-element.15) | copy-start | bytes 786436
  62.2 0.8 %copy-start.4 = (f32[8,4,256]{2,1,0:T(4,128)S(1)}, f32[8,4,256]{2,1,0:T(4,128)}, u32[]{:S(2)}) copy-start(f32[8,4,256]{2,1,0:T(4,128)} %get-tuple-element.16) | copy-start | bytes 98308
  62.2 1.4 %copy-start.3 = (f32[64,512]{1,0:T(8,128)S(1)}, f32[64,512]{1,0:T(8,128)}, u32[]{:S(2)}) copy-start(f32[64,512]{1,0:T(8,128)} %get-tuple-element.17) | copy-start | bytes 393220

commit v4 on v3

--- a/solution.py
+++ b/solution.py
@@ -64,9 +64,9 @@
 
 
 def step_kernel(
-    q_hbm, k_hbm, v_hbm, lam_ref, proj_ref, og_hbm,
+    q_hbm, k_hbm, v_hbm, lam_hbm, proj_hbm, og_hbm,
     out_ref, gq_ref, gk_ref, gv_ref, gl_ref, gp_ref,
-    q, k, v, og, ogt, lamt, glt, glrow, shard_buf, full, states, score, prob, att32, att, mapped, ga, wt, gk32, gv32,
+    q, k, v, og, ogt, lamt, glt, glrow, lam_in, shard_buf, full, states, score, prob, att32, att, mapped, ga, wt, gk32, gv32,
     tot, col, pair, quad, csum, xin, s3buf, s4buf,
     ubuf, ucol, asend, uxin, rsend, rcol, usib,
     g32, gbf, gsib, hbuf, rel, fin, gbuf, xg, zf, zsend, zin, zall,
@@ -87,7 +87,9 @@
 
     loads = [
         pltpu.make_async_copy(src, dst, ld.at[i])
-        for i, (src, dst) in enumerate(((k_hbm, k), (v_hbm, v), (q_hbm, q), (og_hbm, og)))
+        for i, (src, dst) in enumerate(
+            ((k_hbm, k), (v_hbm, v), (q_hbm, q), (og_hbm, og), (proj_hbm, shard_buf), (lam_hbm, lam_in))
+        )
     ]
     for cp in loads:
         cp.start()
@@ -104,10 +106,6 @@
     def lanes(h):
         return pl.ds(128 * h, 128)
 
-    shard_buf[...] = proj_ref[...]
-    for level in range(8):
-        glrow[pl.ds(4 * level, 4)] = lam_ref[level]
-    lamt[...] = glrow[...].T
     loads[0].wait()
     loads[1].wait()
     for h in range(4):
@@ -142,6 +140,7 @@
     def chip(a, b):
         return flipped(s, bits, a << 1 | b << 3)
 
+    loads[4].wait()
     full[rows(s, 64)] = shard_buf[...]
     for a in (1, 3, 2):
         ag(a, shard_buf, s, {"seq": chip(a, 0)})
@@ -176,6 +175,10 @@
             prob[h, 2], v[half(0), lanes(h)], NN
         )
 
+    loads[5].wait()
+    for level in range(8):
+        glrow[pl.ds(4 * level, 4)] = lam_in[level]
+    lamt[...] = glrow[...].T
     loads[2].wait()
     inside(0)
     inside(1)
@@ -269,7 +272,6 @@
 
     first_axis(2)
     second_axis(0)
-    second_axis(1)
 
     inside(3)
     loads[3].wait()
@@ -278,8 +280,7 @@
         ogt[0, n] = turned[:64]
         ogt[1, n] = turned[64:]
 
-    second_axis(3)
-    second_axis(2)
+    second_axis(1)
 
     @pl.when(have[0])
     def _():
@@ -315,9 +316,8 @@
         part = pl.ds(4 * n, 4)
         g32[part] = dot(ogt[c, part].reshape(256, 256), att[...], NN).reshape(4, 64, 512)
 
-    for a in (0, 1, 3, 2):
-        ag_arrived(4 + 4 * a + 2)
-        ag(20 + 4 * a + 2, block(chip(a, 2)), chip(a, 2), sibling)
+    second_axis(3)
+    second_axis(2)
 
     def h_make(a, b):
         slot = 4 * a + b
@@ -349,39 +349,13 @@
     f31 = final(3, 1)
     f31.start()
 
+    for a in (0, 1, 3, 2):
+        ag_arrived(4 + 4 * a + 2)
+        ag(20 + 4 * a + 2, block(chip(a, 2)), chip(a, 2), sibling)
+
     for a in range(4):
         for b in range(4):
             ag_arrived(20 + 4 * a + b)
-    ga[...] = dot(og[...], full[...], NN).astype(BF)
-    for h in range(4):
-        g = ga[:, lanes(h)].astype(F32)
-        for j in range(5):
-            wt[h, j] = (SCALE * lam(3 + j, h, pl.ds(0, 256)) * g).astype(BF)
-            ubuf[j, lanes(h)] = dot(q[:, lanes(h)], wt[h, j], TN).astype(BF)
-
-    usend = send(ubuf.at[0], usib, us_s, us_r, sibling)
-
-    @pl.when(have[0])
-    def _():
-        usend.start()
-
-    def slice_to(j, m):
-        peer = flipped(s, bits, m)
-        return send(
-            ubuf.at[j, rows(lax.rem(peer, COL), 64)],
-            ucol.at[j - 1, m],
-            u_s.at[j - 1, m],
-            u_r.at[j - 1, m],
-            {"seq": peer},
-        )
-
-    for j in (4, 3, 2, 1):
-
-        @pl.when(have[j])
-        def _(j=j):
-            for m in ORDER:
-                slice_to(j, m).start()
-
     for b in range(2):
         h_make(3, b)
     rl[1].wait_recv()
@@ -396,6 +370,36 @@
         hbuf[1, 2 + b] = (hbuf[1, 2 + b].astype(F32) + rel[1, b].astype(F32)).astype(BF)
     f11 = final(1, 1)
     f11.start()
+
+    ga[...] = dot(og[...], full[...], NN).astype(BF)
+    for h in range(4):
+        g = ga[:, lanes(h)].astype(F32)
+        for j in range(5):
+            wt[h, j] = (SCALE * lam(3 + j, h, pl.ds(0, 256)) * g).astype(BF)
+            ubuf[j, lanes(h)] = dot(q[:, lanes(h)], wt[h, j], TN).astype(BF)
+
+    usend = send(ubuf.at[0], usib, us_s, us_r, sibling)
+
+    @pl.when(have[0])
+    def _():
+        usend.start()
+
+    def slice_to(j, m):
+        peer = flipped(s, bits, m)
+        return send(
+            ubuf.at[j, rows(lax.rem(peer, COL), 64)],
+            ucol.at[j - 1, m],
+            u_s.at[j - 1, m],
+            u_r.at[j - 1, m],
+            {"seq": peer},
+        )
+
+    for j in (4, 3, 2, 1):
+
+        @pl.when(have[j])
+        def _(j=j):
+            for m in ORDER:
+                slice_to(j, m).start()
 
     place_of = lax.broadcasted_iota(jnp.int32, (128, 128), 1)
 
@@ -443,40 +447,6 @@
     backward(0)
     backward(1)
 
-    for j in range(1, 5):
-        for m in range(COL):
-            cond = bit_of(bits, j, m) == 1 if j < 3 else have[j]
-
-            @pl.when(cond)
-            def _(j=j, m=m):
-                if m:
-                    slice_to(j, m).wait_recv()
-                else:
-                    ucol[j - 1, 0] = ubuf[j, mine]
-
-            @pl.when(jnp.logical_not(cond))
-            def _(j=j, m=m):
-                ucol[j - 1, m] = jnp.zeros((64, 128), BF)
-
-    def total(j, ms):
-        value = ucol[j - 1, ms[0]].astype(F32)
-        for m in ms[1:]:
-            value = value + ucol[j - 1, m].astype(F32)
-        return value
-
-    asend[0] = total(3, list(range(COL)))
-    asend[1] = total(4, list(range(COL)))
-    ux = [
-        send(asend.at[0 if m == 1 else 1], uxin.at[m], ux_s.at[m], ux_r.at[m], {"seq": flipped(s, bits, m << 3)})
-        for m in range(1, 4)
-    ]
-    ux_out = [x0 == 1, x1 == 1, x1 == 1]
-    for cp, cond in zip(ux, ux_out):
-
-        @pl.when(cond)
-        def _(cp=cp):
-            cp.start()
-
     for b in range(4):
         h_make(0, b)
     for cp in (f10, f31, f30, f11):
@@ -489,30 +459,41 @@
         cp.start()
         gx.append(cp)
 
+    for j in range(1, 5):
+        for m in range(COL):
+            cond = bit_of(bits, j, m) == 1 if j < 3 else have[j]
+
+            @pl.when(cond)
+            def _(j=j, m=m):
+                if m:
+                    slice_to(j, m).wait_recv()
+                else:
+                    ucol[j - 1, 0] = ubuf[j, mine]
+
+            @pl.when(jnp.logical_not(cond))
+            def _(j=j, m=m):
+                ucol[j - 1, m] = jnp.zeros((64, 128), BF)
+
+    def total(j, ms):
+        value = ucol[j - 1, ms[0]].astype(F32)
+        for m in ms[1:]:
+            value = value + ucol[j - 1, m].astype(F32)
+        return value
+
+    asend[0] = total(3, list(range(COL)))
+    asend[1] = total(4, list(range(COL)))
+    ux = [
+        send(asend.at[0 if m == 1 else 1], uxin.at[m], ux_s.at[m], ux_r.at[m], {"seq": flipped(s, bits, m << 3)})
+        for m in range(1, 4)
+    ]
+    ux_out = [x0 == 1, x1 == 1, x1 == 1]
+    for cp, cond in zip(ux, ux_out):
+
+        @pl.when(cond)
+        def _(cp=cp):
+            cp.start()
+
     backward(2)
-
-    for cp, cond, m in zip(ux, ux_out, range(1, 4)):
-
-        @pl.when(jnp.logical_not(cond))
-        def _(cp=cp):
-            cp.wait_recv()
-
-        @pl.when(cond)
-        def _(m=m):
-            uxin[m] = jnp.zeros((64, 128), F32)
-
-    beyond = uxin[1] + uxin[2] + uxin[3]
-    for i in range(4):
-        n = 4 * ((i >> 1) ^ 1)
-        rsend[i] = (
-            beyond + total(1, [2 * (i ^ 1), 2 * (i ^ 1) + 1]) + total(2, [n, n + 1, n + 2, n + 3])
-        ).astype(BF)
-    rc = []
-    for m in ORDER:
-        cp = send(rsend.at[m >> 1], rcol.at[mine], ur_s.at[m], ur_r.at[m], {"seq": flipped(s, bits, m)})
-        cp.start()
-        rc.append(cp)
-    rcol[mine] = rsend[0]
 
     for cp in gx:
         cp.wait_recv()
@@ -528,6 +509,29 @@
         cp.start()
         z1.append(cp)
 
+    for cp, cond, m in zip(ux, ux_out, range(1, 4)):
+
+        @pl.when(jnp.logical_not(cond))
+        def _(cp=cp):
+            cp.wait_recv()
+
+        @pl.when(cond)
+        def _(m=m):
+            uxin[m] = jnp.zeros((64, 128), F32)
+
+    beyond = uxin[1] + uxin[2] + uxin[3]
+    for i in range(4):
+        n = 4 * ((i >> 1) ^ 1)
+        rsend[i] = (
+            beyond + total(1, [2 * (i ^ 1), 2 * (i ^ 1) + 1]) + total(2, [n, n + 1, n + 2, n + 3])
+        ).astype(BF)
+    rc = []
+    for m in ORDER:
+        cp = send(rsend.at[m >> 1], rcol.at[mine], ur_s.at[m], ur_r.at[m], {"seq": flipped(s, bits, m)})
+        cp.start()
+        rc.append(cp)
+    rcol[mine] = rsend[0]
+
     backward(3)
 
     def output(n):
@@ -604,7 +608,7 @@
 
 def step(query, key, value, lam, proj, grad_out):
     dma = pltpu.SemaphoreType.DMA
-    any_space = pl.BlockSpec(memory_space=pl.ANY)
+    outer = pl.BlockSpec(memory_space=pltpu.HBM)
     inner = pl.BlockSpec(memory_space=pltpu.VMEM)
     wide = (256, 512)
     return pl.pallas_call(
@@ -617,7 +621,7 @@
             jax.ShapeDtypeStruct((8, 4, 256), F32),
             jax.ShapeDtypeStruct((64, 512), F32),
         ),
-        in_specs=[any_space, any_space, any_space, inner, inner, any_space],
+        in_specs=[outer] * 6,
         out_specs=(inner,) * 6,
         scratch_shapes=[
             pltpu.VMEM(wide, BF), pltpu.VMEM(wide, BF), pltpu.VMEM(wide, BF),
@@ -626,6 +630,7 @@
             pltpu.VMEM((256, 32), F32),
             pltpu.VMEM((256, 128), F32),
             pltpu.VMEM((32, 256), F32),
+            pltpu.VMEM((8, 4, 256), F32),
             pltpu.VMEM((64, 512), BF),
             pltpu.VMEM((2048, 512), BF),
             pltpu.VMEM((5, 512, 128), BF),
@@ -665,21 +670,48 @@
             pltpu.VMEM((8, 16, 256), BF),
             pltpu.VMEM((8, 16, 256), BF),
             pltpu.VMEM((8, 16, 256), BF),
-            dma((4,)),
+            dma((6,)),
             dma((36,)), dma((36,)), dma((COL,)), dma((COL,)),
             dma((5, COL)), dma((5, COL)), dma((4,)), dma((4,)), dma, dma,
             dma((4, COL)), dma((4, COL)), dma((4,)), dma((4,)), dma((COL,)), dma((COL,)), dma, dma,
             dma((PIECES,)), dma((PIECES,)), dma((2,)), dma((2,)), dma((4,)), dma((4,)),
             dma((4,)), dma((4,)), dma((8,)), dma((8,)), dma((8,)), dma((8,)),
         ],
-        compiler_params=pltpu.CompilerParams(collective_id=0, has_side_effects=True),
+        compiler_params=pltpu.CompilerParams(collective_id=0, has_side_effects=True, vmem_limit_bytes=36 * 2**20),
         name="span_step",
     )(query, key, value, lam, proj, grad_out)
 
 
+def deliver_kernel(*refs):
+    count = len(refs) // 2
+    sems = refs[-1]
+    copies = [pltpu.make_async_copy(refs[i], refs[count + i], sems.at[i]) for i in range(count)]
+    for cp in copies:
+        cp.start()
+    for cp in copies:
+        cp.wait()
+
+
+def deliver(arrays):
+    return pl.pallas_call(
+        deliver_kernel,
+        out_shape=[jax.ShapeDtypeStruct(x.shape, x.dtype) for x in arrays],
+        in_specs=[pl.BlockSpec(memory_space=pltpu.VMEM)] * len(arrays),
+        out_specs=[pl.BlockSpec(memory_space=pltpu.HBM)] * len(arrays),
+        scratch_shapes=[pltpu.SemaphoreType.DMA((len(arrays),))],
+        compiler_params=pltpu.CompilerParams(vmem_limit_bytes=2**20),
+        name="deliver",
+    )(*arrays)
+
+
 def shards(queries, keys, values, level_weights, proj, out_grad):
-    out, gq, gk, gv, gl, gp = step(
-        queries[0], keys[0], values[0], level_weights[0], proj.T, out_grad[0]
+    out, gq, gk, gv, gl, gp = deliver(
+        step(
+            *[
+                pltpu.with_memory_space_constraint(x, pltpu.HBM)
+                for x in (queries[0], keys[0], values[0], level_weights[0], proj.T, out_grad[0])
+            ]
+        )
     )
     return out[None], gq[None], gk[None], gv[None], gl[None], gp.T
 

time: 64.5 us -> 54.6 us (0.85)
  the two profiles are of different devices: /device:TPU:16 before, /device:TPU:8 now
where the time goes in v4:
time: 54.6 us; the launch traced here: 54.1 us
  Pallas kernels  53.5 us (98%)
  between operations  0.64 us (1%)
    pallas_call x1, Pallas kernels, step(): pl.pallas_call(step_kernel, out_shape=(jax.ShapeDtypeStruct((256, 2048),...  52.2 us
    pallas_call x1, Pallas kernels, deliver(): pl.pallas_call(deliver_kernel, out_shape=[jax.ShapeDtypeStruct(x.shape, x...  1.33 us

profile of v4, /device:TPU:8, one launch (start us, length us, event | category | flops | bytes accessed | tf_op | source)
XLA Modules:
  0.0 54.1 jit_solution(16060956590062017099)
XLA Ops:
  0.6 52.2 %span_step.1 = (bf16[256,2048]{1,0:T(8,128)(2,1)S(1)}, bf16[256,512]{1,0:T(8,128)(2,1)S(1)}, bf16[256,512]{1,0:T(8,128)(2,1)S(1)}, bf16[256,512]{1,0:T(8,128)(2,...) custom-call(bf16[256,512]{1,0:T(8,128)(2,1)} %bitcast.13, bf16[256,512]{1,0:T(8,128)(2,1)} %bitcast.14, ...), custom_call_target="tpu_custom_call" | custom-call | tf_op jit(solution)/shard_map/span_step/pallas_call | solution.py:614
  52.8 1.3 %deliver.1 = (bf16[256,2048]{1,0:T(8,128)(2,1)}, bf16[256,512]{1,0:T(8,128)(2,1)}, bf16[256,512]{1,0:T(8,128)(2,1)}, bf16[256,512]{1,0:T(8,128)(2,1)}, f32[8,4,256]{2,1,0:T(4,128)}, /*index=5*/f32[64,512]{1,0:T(8,128)}) custom-call(bf16[256,2048]{1,0:T(8,128)(2,1)S(1)} %get-tuple-element.18.refs_0_, bf16[256,512]{1,0:T(8,128)(2,1)S(1)} %get-tuple-element.19.refs_1_, ...), custom_call_target="tpu_custom_call" | custom-call | tf_op jit(solution)/shard_map/deliver/pallas_call | solution.py:696

commit v5 on v4

--- a/solution.py
+++ b/solution.py
@@ -68,10 +68,10 @@
     out_ref, gq_ref, gk_ref, gv_ref, gl_ref, gp_ref,
     q, k, v, og, ogt, lamt, glt, glrow, lam_in, shard_buf, full, states, score, prob, att32, att, mapped, ga, wt, gk32, gv32,
     tot, col, pair, quad, csum, xin, s3buf, s4buf,
-    ubuf, ucol, asend, uxin, rsend, rcol, usib,
+    ubuf, upre, upsum, ucol, asend, uxin, rsend, rcol, usib,
     g32, gbf, gsib, hbuf, rel, fin, gbuf, xg, zf, zsend, zin, zall,
     ld, ag_s, ag_r, c1_s, c1_r, st_s, st_r, x_s, x_r, sib_s, sib_r,
-    u_s, u_r, ux_s, ux_r, ur_s, ur_r, us_s, us_r,
+    uh_s, uh_r, u_s, u_r, ux_s, ux_r, ur_s, ur_r, us_s, us_r, rj_s, rj_r,
     gs_s, gs_r, rl_s, rl_r, fn_s, fn_r, gx_s, gx_r, z1_s, z1_r, z2_s, z2_r,
 ):
     s, bits = place()
@@ -144,9 +144,32 @@
     full[rows(s, 64)] = shard_buf[...]
     for a in (1, 3, 2):
         ag(a, shard_buf, s, {"seq": chip(a, 0)})
-    for b in (1, 3):
-        ag(4 + b, shard_buf, s, {"seq": chip(0, b)})
     ag(20, shard_buf, s, sibling)
+
+    odd = zbits[0]
+    dz = ({"dp": lax.rem(z + 1, 8)}, {"dp": lax.rem(z + 7, 8)})
+
+    def piece(a, b):
+        turn = 1 - odd if a & 1 else odd
+        return chip(a & 2, b) + 2 * (1 - 2 * y0) * turn
+
+    along = {}
+    for a in (0, 2):
+        for b in (1, 3):
+            slot = 4 + 4 * a + b
+            at = block(piece(a, 0))
+            along[a, b] = send(at, at, ag_s.at[slot], ag_r.at[slot], {"seq": chip(0, b)})
+            open_sends.append(along[a, b])
+
+    def set_out(*labels):
+        for a in labels:
+            along[a, 1].start()
+            along[a, 3].start()
+
+    @pl.when(odd == 0)
+    def _():
+        set_out(0)
+
 
     row = lax.broadcasted_iota(jnp.int32, (128, 128), 0)
     column = lax.broadcasted_iota(jnp.int32, (128, 128), 1)
@@ -209,7 +232,7 @@
         return send(src, states.at[j, mine], st_s.at[j, m], st_r.at[j, m], {"seq": flipped(s, bits, m)})
 
     early = []
-    for m in ORDER:
+    for m in (4, 2, 6, 1):
         early.append((spread(1, m, pair.at[(m >> 1) ^ 1]), bit_of(bits, 1, m) == 1))
         early.append((spread(2, m, quad.at[(m >> 2) ^ 1]), bit_of(bits, 2, m) == 1))
     for cp, cond in early:
@@ -218,6 +241,15 @@
         def _(cp=cp):
             cp.start()
 
+    def hand_over(j, i):
+        at = states.at[j, rows(lax.rem(flipped(s, bits, 2 * i), COL), 64)]
+        return send(at, at, st_s.at[j, 2 * i + 1], st_r.at[j, 2 * i + 1], sibling)
+
+    def handed(j):
+        for i in (2, 1, 3):
+            spread(j, 2 * i, s4buf).wait_recv()
+            hand_over(j, i).start()
+
     for j in range(5):
 
         @pl.when(jnp.logical_not(have[j]))
@@ -234,19 +266,33 @@
 
     def first_axis(a):
         ag_arrived(a)
-        for b in (1, 3):
-            ag(4 + 4 * a + b, block(chip(a, 0)), chip(a, 0), {"seq": chip(0, b)})
         ag(20 + 4 * a, block(chip(a, 0)), chip(a, 0), sibling)
+
+    def pass_on(a, b):
+        ag(36 + 2 * a + b, block(piece(a, b)), piece(a, b), dz[a >> 1])
+        ag(20 + 4 * a + b, block(piece(a, b)), piece(a, b), sibling)
 
     def second_axis(a):
         for b in (1, 3):
             ag_arrived(4 + 4 * a + b)
-            if (b == 1) == (a < 2):
-                ag(4 + 4 * a + 2, block(chip(a, b)), chip(a, b), {"seq": chip(0, 4 - b)})
-            ag(20 + 4 * a + b, block(chip(a, b)), chip(a, b), sibling)
+            if (b == 1) == (a == 0):
+                ag(4 + 4 * a + 2, block(piece(a, b)), piece(a, b), {"seq": chip(0, 4 - b)})
+            pass_on(a, b)
+
+    def far_chip(a):
+        ag_arrived(4 + 4 * a + 2)
+        pass_on(a, 2)
+
+    def other_plane(a, b):
+        ag_arrived(36 + 2 * a + b)
+        ag(24 + 4 * a + b, block(piece(a + 1, b)), piece(a + 1, b), sibling)
 
     first_axis(1)
     first_axis(3)
+
+    @pl.when(odd == 1)
+    def _():
+        set_out(0, 2)
 
     inside(2)
 
@@ -271,26 +317,37 @@
         states[4, mine] = s4buf[...]
 
     first_axis(2)
-    second_axis(0)
+
+    @pl.when(odd == 0)
+    def _():
+        set_out(2)
 
     inside(3)
     loads[3].wait()
-    for n in range(16):
-        turned = og[:, pl.ds(128 * n, 128)].T
-        ogt[0, n] = turned[:64]
-        ogt[1, n] = turned[64:]
-
-    second_axis(1)
-
-    @pl.when(have[0])
-    def _():
-        sib.wait_recv()
-
-    for j in range(1, 5):
+    for a in range(4):
+        for b in range(4):
+            turned = og[:, rows(lax.div(off(a, b), 2), 128)].T
+            ogt[0, a, b] = turned[:64]
+            ogt[1, a, b] = turned[64:]
+
+    for j in (1, 2):
 
         @pl.when(have[j])
         def _(j=j):
-            for m in ORDER:
+            handed(j)
+
+    second_axis(0)
+    second_axis(2)
+
+    @pl.when(have[0])
+    def _():
+        sib.wait_recv()
+
+    for j in range(1, 5):
+
+        @pl.when(have[j])
+        def _(j=j):
+            for m in (1, 3, 5, 7) if j < 3 else ORDER:
                 spread(j, m, s4buf).wait_recv()
 
     for h in range(4):
@@ -301,28 +358,30 @@
             cross = cross + lam(3 + j, h, pl.ds(0, 256)) * image
         att[:, lanes(h)] = (att32[:, lanes(h)] + SCALE * cross).astype(BF)
 
-    other = 1 - c
-    for n in range(4):
-        part = pl.ds(4 * n, 4)
-        gbf[part] = dot(ogt[other, part].reshape(256, 256), att[...], NN).astype(BF).reshape(4, 64, 512)
     gs = []
+
+    def exchange(*firsts):
+        for a in firsts:
+            gbf[a] = dot(ogt[1 - c, a].reshape(256, 256), att[...], NN).astype(BF).reshape(4, 64, 512)
+        for a in firsts:
+            for b in range(4):
+                slot = 4 * b + a
+                cp = send(gbf.at[a, b], gsib.at[slot], gs_s.at[slot], gs_r.at[slot], sibling)
+                cp.start()
+                gs.append(cp)
+
+    exchange(2)
+    exchange(1, 3, 0)
     for a in (2, 1, 3, 0):
-        for b in range(4):
-            slot = 4 * b + a
-            cp = send(gbf.at[lax.div(off(a, b), 2)], gsib.at[slot], gs_s.at[slot], gs_r.at[slot], sibling)
-            cp.start()
-            gs.append(cp)
-    for n in range(4):
-        part = pl.ds(4 * n, 4)
-        g32[part] = dot(ogt[c, part].reshape(256, 256), att[...], NN).reshape(4, 64, 512)
-
-    second_axis(3)
-    second_axis(2)
+        g32[a] = dot(ogt[c, a].reshape(256, 256), att[...], NN).reshape(4, 64, 512)
+
+    far_chip(0)
+    far_chip(2)
 
     def h_make(a, b):
         slot = 4 * a + b
-        send(gbf.at[0], gsib.at[slot], gs_s.at[slot], gs_r.at[slot], sibling).wait_recv()
-        hbuf[a, b] = (g32[lax.div(off(a, b), 2)] + gsib[slot].astype(F32)).astype(BF)
+        send(gbf.at[0, 0], gsib.at[slot], gs_s.at[slot], gs_r.at[slot], sibling).wait_recv()
+        hbuf[a, b] = (g32[a, b] + gsib[slot].astype(F32)).astype(BF)
 
     dev_a = {1: {"seq": off(1, 0)}, 3: {"seq": off(3, 0)}}
     for b in range(4):
@@ -349,13 +408,10 @@
     f31 = final(3, 1)
     f31.start()
 
-    for a in (0, 1, 3, 2):
-        ag_arrived(4 + 4 * a + 2)
-        ag(20 + 4 * a + 2, block(chip(a, 2)), chip(a, 2), sibling)
-
-    for a in range(4):
-        for b in range(4):
-            ag_arrived(20 + 4 * a + b)
+    for b in (1, 3, 2):
+        other_plane(0, b)
+        other_plane(2, b)
+
     for b in range(2):
         h_make(3, b)
     rl[1].wait_recv()
@@ -371,6 +427,9 @@
     f11 = final(1, 1)
     f11.start()
 
+    for a in range(4):
+        for b in range(4):
+            ag_arrived(20 + 4 * a + b)
     ga[...] = dot(og[...], full[...], NN).astype(BF)
     for h in range(4):
         g = ga[:, lanes(h)].astype(F32)
@@ -384,22 +443,34 @@
     def _():
         usend.start()
 
-    def slice_to(j, m):
-        peer = flipped(s, bits, m)
-        return send(
-            ubuf.at[j, rows(lax.rem(peer, COL), 64)],
-            ucol.at[j - 1, m],
-            u_s.at[j - 1, m],
-            u_r.at[j - 1, m],
-            {"seq": peer},
-        )
-
+    y = y0 + 2 * y1
+    kept = rows(c, 256)
+    shared = [
+        send(ubuf.at[j, rows(1 - c, 256)], upre.at[j - 1], uh_s.at[j - 1], uh_r.at[j - 1], sibling)
+        for j in range(1, 5)
+    ]
     for j in (4, 3, 2, 1):
 
         @pl.when(have[j])
         def _(j=j):
-            for m in ORDER:
-                slice_to(j, m).start()
+            shared[j - 1].start()
+
+    def slice_to(j, i):
+        peer = flipped(s, bits, 2 * i)
+        at = rows(lax.div(lax.rem(peer, COL), 2), 64)
+        return send(
+            upsum.at[j - 1, at], ucol.at[j - 1, i], u_s.at[j - 1, i], u_r.at[j - 1, i], {"seq": peer}
+        )
+
+    def spread_updates():
+        for j in (4, 3, 2, 1):
+
+            @pl.when(have[j])
+            def _(j=j):
+                shared[j - 1].wait_recv()
+                upsum[j - 1] = (ubuf[j, kept].astype(F32) + upre[j - 1].astype(F32)).astype(BF)
+                for i in (2, 1, 3):
+                    slice_to(j, i).start()
 
     place_of = lax.broadcasted_iota(jnp.int32, (128, 128), 1)
 
@@ -445,6 +516,9 @@
 
     glt[...] = jnp.zeros_like(glt)
     backward(0)
+
+    spread_updates()
+
     backward(1)
 
     for b in range(4):
@@ -460,28 +534,28 @@
         gx.append(cp)
 
     for j in range(1, 5):
-        for m in range(COL):
-            cond = bit_of(bits, j, m) == 1 if j < 3 else have[j]
+        for i in range(4):
+            cond = bit_of(bits, j, 2 * i) == 1 if j < 3 else have[j]
 
             @pl.when(cond)
-            def _(j=j, m=m):
-                if m:
-                    slice_to(j, m).wait_recv()
+            def _(j=j, i=i):
+                if i:
+                    slice_to(j, i).wait_recv()
                 else:
-                    ucol[j - 1, 0] = ubuf[j, mine]
+                    ucol[j - 1, 0] = upsum[j - 1, rows(y, 64)]
 
             @pl.when(jnp.logical_not(cond))
-            def _(j=j, m=m):
-                ucol[j - 1, m] = jnp.zeros((64, 128), BF)
-
-    def total(j, ms):
-        value = ucol[j - 1, ms[0]].astype(F32)
-        for m in ms[1:]:
-            value = value + ucol[j - 1, m].astype(F32)
+            def _(j=j, i=i):
+                ucol[j - 1, i] = jnp.zeros((64, 128), BF)
+
+    def total(j, chips):
+        value = ucol[j - 1, chips[0]].astype(F32)
+        for i in chips[1:]:
+            value = value + ucol[j - 1, i].astype(F32)
         return value
 
-    asend[0] = total(3, list(range(COL)))
-    asend[1] = total(4, list(range(COL)))
+    asend[0] = total(3, [0, 1, 2, 3])
+    asend[1] = total(4, [0, 1, 2, 3])
     ux = [
         send(asend.at[0 if m == 1 else 1], uxin.at[m], ux_s.at[m], ux_r.at[m], {"seq": flipped(s, bits, m << 3)})
         for m in range(1, 4)
@@ -521,16 +595,15 @@
 
     beyond = uxin[1] + uxin[2] + uxin[3]
     for i in range(4):
-        n = 4 * ((i >> 1) ^ 1)
-        rsend[i] = (
-            beyond + total(1, [2 * (i ^ 1), 2 * (i ^ 1) + 1]) + total(2, [n, n + 1, n + 2, n + 3])
-        ).astype(BF)
+        n = 2 * ((i >> 1) ^ 1)
+        rsend[i] = (beyond + total(1, [i ^ 1]) + total(2, [n, n + 1])).astype(BF)
+    owned = rows(4 * c + y, 64)
     rc = []
-    for m in ORDER:
-        cp = send(rsend.at[m >> 1], rcol.at[mine], ur_s.at[m], ur_r.at[m], {"seq": flipped(s, bits, m)})
+    for i in (2, 1, 3):
+        cp = send(rsend.at[i], rcol.at[owned], ur_s.at[i], ur_r.at[i], {"seq": flipped(s, bits, 2 * i)})
         cp.start()
         rc.append(cp)
-    rcol[mine] = rsend[0]
+    rcol[owned] = rsend[0]
 
     backward(3)
 
@@ -554,10 +627,15 @@
         z2.append(cp)
 
     output(2)
-    output(3)
 
     for cp in rc:
         cp.wait_recv()
+    join = send(rcol.at[kept], rcol.at[kept], rj_s, rj_r, sibling)
+    join.start()
+
+    output(3)
+
+    join.wait_recv()
 
     @pl.when(c == 0)
     def _():
@@ -580,7 +658,7 @@
     for i in range(8):
         gp_ref[pl.ds(16 * (i // 2), 16), pl.ds(256 * (i % 2), 256)] = zall[i].astype(F32)
 
-    for cp in first + open_sends + gs + [rl[1], rl[3], f10, f11, f30, f31] + rc + gx + z1 + z2:
+    for cp in first + open_sends + gs + [rl[1], rl[3], f10, f11, f30, f31, join] + rc + gx + z1 + z2:
         cp.wait_send()
     for cp, cond in early + list(zip(xsend, x_out)) + list(zip(ux, ux_out)):
 
@@ -600,9 +678,10 @@
 
         @pl.when(have[j])
         def _(j=j):
-            for m in ORDER:
-                slice_to(j, m).wait_send()
-            for cp in {3: late3, 4: late4}.get(j, []):
+            shared[j - 1].wait_send()
+            for i in (2, 1, 3):
+                slice_to(j, i).wait_send()
+            for cp in {3: late3, 4: late4}.get(j) or [hand_over(j, i) for i in (2, 1, 3)]:
                 cp.wait_send()
 
 
@@ -626,7 +705,7 @@
         scratch_shapes=[
             pltpu.VMEM(wide, BF), pltpu.VMEM(wide, BF), pltpu.VMEM(wide, BF),
             pltpu.VMEM((256, 2048), BF),
-            pltpu.VMEM((2, PIECES, 64, 256), BF),
+            pltpu.VMEM((2, 4, 4, 64, 256), BF),
             pltpu.VMEM((256, 32), F32),
             pltpu.VMEM((256, 128), F32),
             pltpu.VMEM((32, 256), F32),
@@ -652,14 +731,16 @@
             pltpu.VMEM((64, 128), BF),
             pltpu.VMEM((64, 128), BF),
             pltpu.VMEM((5, 512, 128), BF),
-            pltpu.VMEM((4, COL, 64, 128), BF),
+            pltpu.VMEM((4, 256, 128), BF),
+            pltpu.VMEM((4, 256, 128), BF),
+            pltpu.VMEM((4, 4, 64, 128), BF),
             pltpu.VMEM((2, 64, 128), F32),
             pltpu.VMEM((4, 64, 128), F32),
             pltpu.VMEM((4, 64, 128), BF),
             pltpu.VMEM((512, 128), BF),
             pltpu.VMEM((512, 128), BF),
-            pltpu.VMEM((PIECES, 64, 512), F32),
-            pltpu.VMEM((PIECES, 64, 512), BF),
+            pltpu.VMEM((4, 4, 64, 512), F32),
+            pltpu.VMEM((4, 4, 64, 512), BF),
             pltpu.VMEM((PIECES, 64, 512), BF),
             pltpu.VMEM((4, 4, 64, 512), BF),
             pltpu.VMEM((2, 2, 64, 512), BF),
@@ -671,9 +752,9 @@
             pltpu.VMEM((8, 16, 256), BF),
             pltpu.VMEM((8, 16, 256), BF),
             dma((6,)),
-            dma((36,)), dma((36,)), dma((COL,)), dma((COL,)),
+            dma((44,)), dma((44,)), dma((COL,)), dma((COL,)),
             dma((5, COL)), dma((5, COL)), dma((4,)), dma((4,)), dma, dma,
-            dma((4, COL)), dma((4, COL)), dma((4,)), dma((4,)), dma((COL,)), dma((COL,)), dma, dma,
+            dma((4,)), dma((4,)), dma((4, 4)), dma((4, 4)), dma((4,)), dma((4,)), dma((4,)), dma((4,)), dma, dma, dma, dma,
             dma((PIECES,)), dma((PIECES,)), dma((2,)), dma((2,)), dma((4,)), dma((4,)),
             dma((4,)), dma((4,)), dma((8,)), dma((8,)), dma((8,)), dma((8,)),
         ],

time: 54.6 us -> 52.7 us (0.965)
  Pallas kernels: 53.5 us -> 51.2 us
    pallas_call x1, Pallas kernels: 52.2 us -> 49.9 us  [step(): pl.pallas_call(step_kernel, out_shape=(jax.ShapeDtypeStruct((256, 2048),...]
where the time goes in v5:
time: 52.7 us; the launch traced here: 51.9 us
  Pallas kernels  51.2 us (97%)
  between operations  0.64 us (1%)
    pallas_call x1, Pallas kernels, step(): pl.pallas_call(step_kernel, out_shape=(jax.ShapeDtypeStruct((256, 2048),...  49.9 us
    pallas_call x1, Pallas kernels, deliver(): pl.pallas_call(deliver_kernel, out_shape=[jax.ShapeDtypeStruct(x.shape, x...  1.33 us

profile of v5, /device:TPU:8, one launch (start us, length us, event | category | flops | bytes accessed | tf_op | source)
XLA Modules:
  0.0 51.9 jit_solution(16989580677353451945)
XLA Ops:
  0.6 49.9 %span_step.1 = (bf16[256,2048]{1,0:T(8,128)(2,1)S(1)}, bf16[256,512]{1,0:T(8,128)(2,1)S(1)}, bf16[256,512]{1,0:T(8,128)(2,1)S(1)}, bf16[256,512]{1,0:T(8,128)(2,...) custom-call(bf16[256,512]{1,0:T(8,128)(2,1)} %bitcast.13, bf16[256,512]{1,0:T(8,128)(2,1)} %bitcast.14, ...), custom_call_target="tpu_custom_call" | custom-call | tf_op jit(solution)/shard_map/span_step/pallas_call | solution.py:693
  50.6 1.3 %deliver.1 = (bf16[256,2048]{1,0:T(8,128)(2,1)}, bf16[256,512]{1,0:T(8,128)(2,1)}, bf16[256,512]{1,0:T(8,128)(2,1)}, bf16[256,512]{1,0:T(8,128)(2,1)}, f32[8,4,256]{2,1,0:T(4,128)}, /*index=5*/f32[64,512]{1,0:T(8,128)}) custom-call(bf16[256,2048]{1,0:T(8,128)(2,1)S(1)} %get-tuple-element.18.refs_0_, bf16[256,512]{1,0:T(8,128)(2,1)S(1)} %get-tuple-element.19.refs_1_, ...), custom_call_target="tpu_custom_call" | custom-call | tf_op jit(solution)/shard_map/deliver/pallas_call | solution.py:777

commit v6 on v5

--- a/solution.py
+++ b/solution.py
@@ -71,7 +71,7 @@
     ubuf, upre, upsum, ucol, asend, uxin, rsend, rcol, usib,
     g32, gbf, gsib, hbuf, rel, fin, gbuf, xg, zf, zsend, zin, zall,
     ld, ag_s, ag_r, c1_s, c1_r, st_s, st_r, x_s, x_r, sib_s, sib_r,
-    uh_s, uh_r, u_s, u_r, ux_s, ux_r, ur_s, ur_r, us_s, us_r, rj_s, rj_r,
+    uh_s, uh_r, u_s, u_r, ux_s, ux_r, ur_s, ur_r, us_s, us_r,
     gs_s, gs_r, rl_s, rl_r, fn_s, fn_r, gx_s, gx_r, z1_s, z1_r, z2_s, z2_r,
 ):
     s, bits = place()
@@ -142,9 +142,8 @@
 
     loads[4].wait()
     full[rows(s, 64)] = shard_buf[...]
-    for a in (1, 3, 2):
-        ag(a, shard_buf, s, {"seq": chip(a, 0)})
-    ag(20, shard_buf, s, sibling)
+    starts = {a: send(shard_buf, block(s), ag_s.at[a], ag_r.at[a], {"seq": chip(a, 0)}) for a in (1, 3, 2)}
+    open_sends.extend(starts.values())
 
     odd = zbits[0]
     dz = ({"dp": lax.rem(z + 1, 8)}, {"dp": lax.rem(z + 7, 8)})
@@ -168,7 +167,16 @@
 
     @pl.when(odd == 0)
     def _():
+        for a in (2, 1, 3):
+            starts[a].start()
         set_out(0)
+
+    @pl.when(odd == 1)
+    def _():
+        for a in (1, 3, 2):
+            starts[a].start()
+
+    ag(20, shard_buf, s, sibling)
 
 
     row = lax.broadcasted_iota(jnp.int32, (128, 128), 0)
@@ -264,10 +272,6 @@
     def _():
         states[2, mine] = quad[1]
 
-    def first_axis(a):
-        ag_arrived(a)
-        ag(20 + 4 * a, block(chip(a, 0)), chip(a, 0), sibling)
-
     def pass_on(a, b):
         ag(36 + 2 * a + b, block(piece(a, b)), piece(a, b), dz[a >> 1])
         ag(20 + 4 * a + b, block(piece(a, b)), piece(a, b), sibling)
@@ -287,12 +291,16 @@
         ag_arrived(36 + 2 * a + b)
         ag(24 + 4 * a + b, block(piece(a + 1, b)), piece(a + 1, b), sibling)
 
-    first_axis(1)
-    first_axis(3)
-
     @pl.when(odd == 1)
     def _():
+        ag_arrived(1)
+        ag_arrived(3)
         set_out(0, 2)
+
+    @pl.when(odd == 0)
+    def _():
+        ag_arrived(2)
+        set_out(2)
 
     inside(2)
 
@@ -316,11 +324,17 @@
             cp.start()
         states[4, mine] = s4buf[...]
 
-    first_axis(2)
+    @pl.when(odd == 1)
+    def _():
+        ag_arrived(2)
 
     @pl.when(odd == 0)
     def _():
-        set_out(2)
+        ag_arrived(1)
+        ag_arrived(3)
+
+    for a in (1, 3, 2):
+        ag(20 + 4 * a, block(chip(a, 0)), chip(a, 0), sibling)
 
     inside(3)
     loads[3].wait()
@@ -384,48 +398,35 @@
         hbuf[a, b] = (g32[a, b] + gsib[slot].astype(F32)).astype(BF)
 
     dev_a = {1: {"seq": off(1, 0)}, 3: {"seq": off(3, 0)}}
-    for b in range(4):
+    relayed = []
+    for b in (0, 2, 1, 3):
         h_make(2, b)
-    rl = {
-        1: send(hbuf.at[2, pl.ds(0, 2)], rel.at[0], rl_s.at[0], rl_r.at[0], dev_a[1]),
-        3: send(hbuf.at[2, pl.ds(2, 2)], rel.at[1], rl_s.at[1], rl_r.at[1], dev_a[3]),
-    }
-    rl[1].start()
-    rl[3].start()
-
-    def final(m, part):
-        n = 2 * (m // 2) + part
-        return send(
-            hbuf.at[m, pl.ds(2 * part, 2)], fin.at[m // 2, pl.ds(2 * part, 2)], fn_s.at[n], fn_r.at[n], dev_a[m]
-        )
-
-    h_make(1, 0)
-    h_make(1, 1)
-    f10 = final(1, 0)
-    f10.start()
-    h_make(3, 2)
-    h_make(3, 3)
-    f31 = final(3, 1)
-    f31.start()
+        cp = send(hbuf.at[2, b], rel.at[b], rl_s.at[b], rl_r.at[b], dev_a[1 if b < 2 else 3])
+        cp.start()
+        relayed.append(cp)
+
+    finals = []
+
+    def final(m, b):
+        n = 4 * (m // 2) + b
+        cp = send(hbuf.at[m, b], fin.at[m // 2, b], fn_s.at[n], fn_r.at[n], dev_a[m])
+        cp.start()
+        finals.append(cp)
+
+    for m, b in ((1, 0), (3, 2), (1, 1), (3, 3)):
+        h_make(m, b)
+        final(m, b)
+    for m, b in ((3, 0), (1, 2), (3, 1), (1, 3)):
+        h_make(m, b)
 
     for b in (1, 3, 2):
         other_plane(0, b)
         other_plane(2, b)
 
-    for b in range(2):
-        h_make(3, b)
-    rl[1].wait_recv()
-    for b in range(2):
-        hbuf[3, b] = (hbuf[3, b].astype(F32) + rel[0, b].astype(F32)).astype(BF)
-    f30 = final(3, 0)
-    f30.start()
-    for b in range(2):
-        h_make(1, 2 + b)
-    rl[3].wait_recv()
-    for b in range(2):
-        hbuf[1, 2 + b] = (hbuf[1, 2 + b].astype(F32) + rel[1, b].astype(F32)).astype(BF)
-    f11 = final(1, 1)
-    f11.start()
+    for m, b, cp in zip((3, 1, 3, 1), (0, 2, 1, 3), relayed):
+        cp.wait_recv()
+        hbuf[m, b] = (hbuf[m, b].astype(F32) + rel[b].astype(F32)).astype(BF)
+        final(m, b)
 
     for a in range(4):
         for b in range(4):
@@ -523,7 +524,7 @@
 
     for b in range(4):
         h_make(0, b)
-    for cp in (f10, f31, f30, f11):
+    for cp in finals:
         cp.wait_recv()
     for b in range(4):
         gbuf[b] = (hbuf[0, b].astype(F32) + fin[0, b].astype(F32) + fin[1, b].astype(F32)).astype(BF)
@@ -532,6 +533,8 @@
         cp = send(gbuf.at[b], xg.at[b], gx_s.at[b], gx_r.at[b], {"seq": off(0, b)})
         cp.start()
         gx.append(cp)
+
+    backward(2)
 
     for j in range(1, 5):
         for i in range(4):
@@ -566,8 +569,6 @@
         @pl.when(cond)
         def _(cp=cp):
             cp.start()
-
-    backward(2)
 
     for cp in gx:
         cp.wait_recv()
@@ -583,6 +584,15 @@
         cp.start()
         z1.append(cp)
 
+    backward(3)
+
+    def output(n):
+        at = pl.ds(512 * n, 512)
+        out_ref[:, at] = dot(att[...], full[at], NT).astype(BF)
+
+    output(0)
+    output(1)
+
     for cp, cond, m in zip(ux, ux_out, range(1, 4)):
 
         @pl.when(jnp.logical_not(cond))
@@ -599,20 +609,11 @@
         rsend[i] = (beyond + total(1, [i ^ 1]) + total(2, [n, n + 1])).astype(BF)
     owned = rows(4 * c + y, 64)
     rc = []
-    for i in (2, 1, 3):
-        cp = send(rsend.at[i], rcol.at[owned], ur_s.at[i], ur_r.at[i], {"seq": flipped(s, bits, 2 * i)})
+    for m in ORDER:
+        cp = send(rsend.at[m >> 1], rcol.at[owned], ur_s.at[m], ur_r.at[m], {"seq": flipped(s, bits, m)})
         cp.start()
         rc.append(cp)
     rcol[owned] = rsend[0]
-
-    backward(3)
-
-    def output(n):
-        at = pl.ds(512 * n, 512)
-        out_ref[:, at] = dot(att[...], full[at], NT).astype(BF)
-
-    output(0)
-    output(1)
 
     for cp in z1:
         cp.wait_recv()
@@ -628,14 +629,10 @@
 
     output(2)
 
+    output(3)
+
     for cp in rc:
         cp.wait_recv()
-    join = send(rcol.at[kept], rcol.at[kept], rj_s, rj_r, sibling)
-    join.start()
-
-    output(3)
-
-    join.wait_recv()
 
     @pl.when(c == 0)
     def _():
@@ -658,7 +655,7 @@
     for i in range(8):
         gp_ref[pl.ds(16 * (i // 2), 16), pl.ds(256 * (i % 2), 256)] = zall[i].astype(F32)
 
-    for cp in first + open_sends + gs + [rl[1], rl[3], f10, f11, f30, f31, join] + rc + gx + z1 + z2:
+    for cp in first + open_sends + gs + relayed + finals + rc + gx + z1 + z2:
         cp.wait_send()
     for cp, cond in early + list(zip(xsend, x_out)) + list(zip(ux, ux_out)):
 
@@ -743,7 +740,7 @@
             pltpu.VMEM((4, 4, 64, 512), BF),
             pltpu.VMEM((PIECES, 64, 512), BF),
             pltpu.VMEM((4, 4, 64, 512), BF),
-            pltpu.VMEM((2, 2, 64, 512), BF),
+            pltpu.VMEM((4, 64, 512), BF),
             pltpu.VMEM((2, 4, 64, 512), BF),
             pltpu.VMEM((4, 64, 512), BF),
             pltpu.VMEM((4, 64, 512), BF),
@@ -754,8 +751,8 @@
             dma((6,)),
             dma((44,)), dma((44,)), dma((COL,)), dma((COL,)),
             dma((5, COL)), dma((5, COL)), dma((4,)), dma((4,)), dma, dma,
-            dma((4,)), dma((4,)), dma((4, 4)), dma((4, 4)), dma((4,)), dma((4,)), dma((4,)), dma((4,)), dma, dma, dma, dma,
-            dma((PIECES,)), dma((PIECES,)), dma((2,)), dma((2,)), dma((4,)), dma((4,)),
+            dma((4,)), dma((4,)), dma((4, 4)), dma((4, 4)), dma((4,)), dma((4,)), dma((COL,)), dma((COL,)), dma, dma,
+            dma((PIECES,)), dma((PIECES,)), dma((4,)), dma((4,)), dma((8,)), dma((8,)),
             dma((4,)), dma((4,)), dma((8,)), dma((8,)), dma((8,)), dma((8,)),
         ],
         compiler_params=pltpu.CompilerParams(collective_id=0, has_side_effects=True, vmem_limit_bytes=36 * 2**20),

time: 52.7 us -> 52.1 us (0.989); the launches traced: 51.9 us -> 51.9 us
  no operation moved by 1% of the time
where the time goes in v6:
time: 52.1 us; the launch traced here: 51.9 us
  Pallas kernels  51.2 us (98%)
  between operations  0.64 us (1%)
    pallas_call x1, Pallas kernels, step(): pl.pallas_call(step_kernel, out_shape=(jax.ShapeDtypeStruct((256, 2048),...  49.9 us
    pallas_call x1, Pallas kernels, deliver(): pl.pallas_call(deliver_kernel, out_shape=[jax.ShapeDtypeStruct(x.shape, x...  1.33 us

profile of v6, /device:TPU:8, one launch (start us, length us, event | category | flops | bytes accessed | tf_op | source)
XLA Modules:
  0.0 51.9 jit_solution(4221967158119638836)
XLA Ops:
  0.6 49.9 %span_step.1 = (bf16[256,2048]{1,0:T(8,128)(2,1)S(1)}, bf16[256,512]{1,0:T(8,128)(2,1)S(1)}, bf16[256,512]{1,0:T(8,128)(2,1)S(1)}, bf16[256,512]{1,0:T(8,128)(2,...) custom-call(bf16[256,512]{1,0:T(8,128)(2,1)} %bitcast.13, bf16[256,512]{1,0:T(8,128)(2,1)} %bitcast.14, ...), custom_call_target="tpu_custom_call" | custom-call | tf_op jit(solution)/shard_map/span_step/pallas_call | solution.py:690
  50.5 1.3 %deliver.1 = (bf16[256,2048]{1,0:T(8,128)(2,1)}, bf16[256,512]{1,0:T(8,128)(2,1)}, bf16[256,512]{1,0:T(8,128)(2,1)}, bf16[256,512]{1,0:T(8,128)(2,1)}, f32[8,4,256]{2,1,0:T(4,128)}, /*index=5*/f32[64,512]{1,0:T(8,128)}) custom-call(bf16[256,2048]{1,0:T(8,128)(2,1)S(1)} %get-tuple-element.18.refs_0_, bf16[256,512]{1,0:T(8,128)(2,1)S(1)} %get-tuple-element.19.refs_1_, ...), custom_call_target="tpu_custom_call" | custom-call | tf_op jit(solution)/shard_map/deliver/pallas_call | solution.py:774

commit v7 on v6

--- a/solution.py
+++ b/solution.py
@@ -91,8 +91,8 @@
             ((k_hbm, k), (v_hbm, v), (q_hbm, q), (og_hbm, og), (proj_hbm, shard_buf), (lam_hbm, lam_in))
         )
     ]
-    for cp in loads:
-        cp.start()
+    for i in (0, 1, 4, 5, 2):
+        loads[i].start()
 
     greeted = (
         [{"seq": flipped(s, bits, m)} for m in range(1, 8)]
@@ -112,6 +112,7 @@
         tot[lanes(h)] = dot(k[:, lanes(h)], v[:, lanes(h)], TN).astype(BF)
     pl.semaphore_wait(barrier, len(greeted))
 
+    loads[3].start()
     first = []
     for m in ORDER:
         peer = flipped(s, bits, m)
@@ -341,8 +342,8 @@
     for a in range(4):
         for b in range(4):
             turned = og[:, rows(lax.div(off(a, b), 2), 128)].T
-            ogt[0, a, b] = turned[:64]
-            ogt[1, a, b] = turned[64:]
+            ogt[0, 0, a, b] = ogt[1, 0, b, a] = turned[:64]
+            ogt[0, 1, a, b] = ogt[1, 1, b, a] = turned[64:]
 
     for j in (1, 2):
 
@@ -374,20 +375,23 @@
 
     gs = []
 
-    def exchange(*firsts):
-        for a in firsts:
-            gbf[a] = dot(ogt[1 - c, a].reshape(256, 256), att[...], NN).astype(BF).reshape(4, 64, 512)
-        for a in firsts:
-            for b in range(4):
+    def exchange(*groups):
+        for b in groups:
+            gbf[b] = dot(ogt[1, 1 - c, b].reshape(256, 256), att[...], NN).astype(BF).reshape(4, 64, 512)
+        for b in groups:
+            for a in range(4):
                 slot = 4 * b + a
-                cp = send(gbf.at[a, b], gsib.at[slot], gs_s.at[slot], gs_r.at[slot], sibling)
+                cp = send(gbf.at[b, a], gsib.at[slot], gs_s.at[slot], gs_r.at[slot], sibling)
                 cp.start()
                 gs.append(cp)
 
     exchange(2)
-    exchange(1, 3, 0)
-    for a in (2, 1, 3, 0):
-        g32[a] = dot(ogt[c, a].reshape(256, 256), att[...], NN).reshape(4, 64, 512)
+    exchange(1, 3)
+
+    def keep(a):
+        g32[a] = dot(ogt[0, c, a].reshape(256, 256), att[...], NN).reshape(4, 64, 512)
+
+    keep(2)
 
     far_chip(0)
     far_chip(2)
@@ -405,6 +409,10 @@
         cp.start()
         relayed.append(cp)
 
+    keep(1)
+    keep(3)
+    exchange(0)
+    keep(0)
     finals = []
 
     def final(m, b):
@@ -702,7 +710,7 @@
         scratch_shapes=[
             pltpu.VMEM(wide, BF), pltpu.VMEM(wide, BF), pltpu.VMEM(wide, BF),
             pltpu.VMEM((256, 2048), BF),
-            pltpu.VMEM((2, 4, 4, 64, 256), BF),
+            pltpu.VMEM((2, 2, 4, 4, 64, 256), BF),
             pltpu.VMEM((256, 32), F32),
             pltpu.VMEM((256, 128), F32),
             pltpu.VMEM((32, 256), F32),

time: 52.1 us -> 50.7 us (0.973)
  Pallas kernels: 51.2 us -> 50 us
    pallas_call x1, Pallas kernels: 49.9 us -> 48.7 us  [step(): pl.pallas_call(step_kernel, out_shape=(jax.ShapeDtypeStruct((256, 2048),...]
where the time goes in v7:
time: 50.7 us; the launch traced here: 50.6 us
  Pallas kernels  50 us (99%)
  between operations  0.64 us (1%)
    pallas_call x1, Pallas kernels, step(): pl.pallas_call(step_kernel, out_shape=(jax.ShapeDtypeStruct((256, 2048),...  48.7 us
    pallas_call x1, Pallas kernels, deliver(): pl.pallas_call(deliver_kernel, out_shape=[jax.ShapeDtypeStruct(x.shape, x...  1.33 us

profile of v7, /device:TPU:8, one launch (start us, length us, event | category | flops | bytes accessed | tf_op | source)
XLA Modules:
  0.0 50.6 jit_solution(6063941881301169327)
XLA Ops:
  0.6 48.7 %span_step.1 = (bf16[256,2048]{1,0:T(8,128)(2,1)S(1)}, bf16[256,512]{1,0:T(8,128)(2,1)S(1)}, bf16[256,512]{1,0:T(8,128)(2,1)S(1)}, bf16[256,512]{1,0:T(8,128)(2,...) custom-call(bf16[256,512]{1,0:T(8,128)(2,1)} %bitcast.13, bf16[256,512]{1,0:T(8,128)(2,1)} %bitcast.14, ...), custom_call_target="tpu_custom_call" | custom-call | tf_op jit(solution)/shard_map/span_step/pallas_call | solution.py:698
  49.3 1.3 %deliver.1 = (bf16[256,2048]{1,0:T(8,128)(2,1)}, bf16[256,512]{1,0:T(8,128)(2,1)}, bf16[256,512]{1,0:T(8,128)(2,1)}, bf16[256,512]{1,0:T(8,128)(2,1)}, f32[8,4,256]{2,1,0:T(4,128)}, /*index=5*/f32[64,512]{1,0:T(8,128)}) custom-call(bf16[256,2048]{1,0:T(8,128)(2,1)S(1)} %get-tuple-element.18.refs_0_, bf16[256,512]{1,0:T(8,128)(2,1)S(1)} %get-tuple-element.19.refs_1_, ...), custom_call_target="tpu_custom_call" | custom-call | tf_op jit(solution)/shard_map/deliver/pallas_call | solution.py:782
